TPU v7x, 128 devices: a whole 4x4x4 slice. The times are simulated.
128 devices in a mesh: freq: 4 (over x_hi, core), gblk: 32 (over x_lo, z, y).
Axes of the slice: x: 4 (x_hi: 2, x_lo: 2; x = x_hi * 2 + x_lo), y: 4, z: 4, core: 2. Of those that a mesh axis runs over, the one named last changes fastest.
Arguments:
- w_imag: bfloat16 [8, 8192, 16384], P('freq', 'gblk'), may hold values from -0.046875 to 0.046875
- w_real: bfloat16 [4, 8192, 16384], P('freq', 'gblk'), may hold values from -0.046875 to 0.046875
- pair_elements: bfloat16 [8192, 256], P('gblk'), may hold values from -1 to 1
- quad_weight: float32 [8, 128], P('freq'), may hold values from 0.1 to 1
- residue_freq: int32 [128], replicated, may hold values from 0 to 3
- owner_bands: int32 [128], replicated, may hold values from 0 to 127, each once
Outputs:
- sigma: float32 [128, 256], P(('freq', 'gblk'))
Inputs may be any that keep to these rules, and one draw needn't show every extreme that they name: `owner_bands`: each band appears once.
All inputs are finite; a program needn't handle non-finite values.
Results may differ from a plain program's by a relative error of at most 0.0003.
Values may be sent and summed in bfloat16 or wider, within the bound.
No kernel may reach another device: no remote copies, remote signals or barrier semaphores. Data moves between devices by JAX's collectives and lax.ppermute only.
A program may use at most 128 MiB of HBM per device.

v0:
```python
import jax
import jax.numpy as jnp
from jax import lax
from jax.sharding import Mesh
from jax.sharding import PartitionSpec as P

GBLK = ("gblk_0", "gblk_1", "gblk_2")
FREQ_GBLK = ("freq", "gblk_0", "gblk_1", "gblk_2")


def joined_along(parts, dim):
    dims = list(parts.shape[1:])
    dims[dim] *= parts.shape[0]
    return jnp.moveaxis(parts, 0, dim).reshape(dims)


def all_blocks(x, axes, sequence):
    parts = x
    for k in sequence:
        parts = lax.all_gather(parts, axes[k])
    done = sequence[::-1]
    back = [done.index(k) for k in range(len(axes))]
    parts = parts.transpose(*back, *range(len(axes), parts.ndim))
    return parts.reshape(-1, *x.shape)


def gather_axes(x, axes, sequence, dim):
    return joined_along(all_blocks(x, axes, sequence), dim)


def split_up(x, dim, size):
    before, after = (x.shape[:dim], x.shape[dim + 1 :])
    return jnp.moveaxis(x.reshape(*before, size, -1, *after), dim, 0)


def summed_on_arrival(x, axis, dim):
    parts = split_up(x, dim, lax.axis_size(axis))
    arrived = lax.all_to_all(parts, axis, split_axis=0, concat_axis=0, tiled=True)
    return arrived.sum(axis=0)


def on_device(w_imag, w_real, pair_elements, quad_weight, residue_freq, owner_bands):
    bands = pair_elements.shape[1] // 2
    g_count = w_imag.shape[2] // 2
    fr_local = w_real.shape[0]
    wide_elems = pair_elements.astype(jnp.float32)
    freq_first_index = lax.axis_index("freq") * fr_local
    real_ids = freq_first_index + jnp.arange(fr_local, dtype=jnp.int32)
    residue_weight = (residue_freq[None, :] == real_ids[:, None]).astype(jnp.float32)
    shard_rows = gather_axes(pair_elements, GBLK, (0, 1, 2), 0)
    row_span = shard_rows.shape[0]
    lower_rows = jnp.concatenate([-shard_rows[:, bands:], shard_rows[:, :bands]], axis=1)

    def contrib(matrix):
        upper_cols = lax.slice_in_dim(matrix, 0, row_span, axis=2)
        lower_cols = lax.dynamic_slice_in_dim(matrix, g_count, row_span, 2)
        result = jnp.einsum(
            "frg,gc->frc", upper_cols, shard_rows, preferred_element_type=jnp.float32
        )
        return result + jnp.einsum(
            "frg,gc->frc", lower_cols, lower_rows, preferred_element_type=jnp.float32
        )

    x_imag = contrib(w_imag)
    x_real = contrib(w_real)

    def sandwich(products):
        blocks = jnp.einsum("gb,fgc->fbc", wide_elems, products, precision=lax.Precision.HIGHEST)
        sig_re = blocks[:, :bands, :bands] + blocks[:, bands:, bands:]
        sig_im = blocks[:, :bands, bands:] - blocks[:, bands:, :bands]
        return jnp.concatenate([sig_re, sig_im], axis=2)

    partial_value = jnp.sum(quad_weight[:, :, None] * sandwich(x_imag), axis=0)
    partial_value = partial_value + jnp.sum(residue_weight[:, :, None] * sandwich(x_real), axis=0)
    onehot = (owner_bands[:, None] == jnp.arange(bands, dtype=jnp.int32)[None, :]).astype(
        jnp.float32
    )
    permuted = jnp.dot(onehot, partial_value, precision=lax.Precision.HIGHEST)
    grouped = summed_on_arrival(permuted, "freq", 0)
    sigma = summed_on_arrival(grouped, GBLK, 0)
    return sigma


def solution(mesh):
    torus = Mesh(
        mesh.devices.reshape(mesh.shape["freq"], 2, 4, 4), ("freq", "gblk_0", "gblk_1", "gblk_2")
    )
    placed = (
        P("freq", GBLK, None),
        P("freq", GBLK, None),
        P(GBLK, None),
        P("freq", None),
        P(),
        P(),
    )
    return jax.shard_map(
        on_device, mesh=torus, in_specs=placed, out_specs=P(FREQ_GBLK, None), check_vma=False
    )
```

profile of v0, /device:TPU:0, one launch (start us, length us, event | category | flops | bytes accessed | tf_op | source)
XLA Modules:
  0.0 157.5 jit_solution(4276669552074100076)
XLA Ops:
  6.5 7.6 %all-gather = bf16[512,256]{1,0:T(8,128)(2,1)} all-gather(bf16[256,256]{1,0:T(8,128)(2,1)} %param.8), channel_id=2, replica_groups=mesh['freq'=4,'gblk_0'=2,'gblk_1'=4,'gblk_2'=4] {'gblk_0'}, dimensions={0}, use_global_device_ids=true | all-gather | bytes 393216 | tf_op jit(solution)/shard_map/all_gather | solution.py:20
  14.2 0.0 all-gather.6.cloned.1.call-update
  14.2 0.0 all-gather.8.cloned.1.call-start
  14.2 26.5 %all-gather.6.cloned.1.call-done = bf16[8,256,256]{2,1,0:T(8,128)(2,1)} async-done(((bf16[2,256,256]{2,1,0:T(8,128)(2,1)}), bf16[8,256,256]{2,1,0:T(8,128)(2,1)}) %all-gather.6.cloned.1.call-update) | async-done | bytes 1048592 | tf_op jit(solution)/shard_map/all_gather | solution.py:20
  40.8 0.7 eq.40
  41.5 0.7 compare_convert_fusion
  42.2 48.7 %all-gather.8.cloned.1.call-done = bf16[16,2,256,256]{3,2,1,0:T(8,128)(2,1)} async-done(((bf16[4,2,256,256]{3,2,1,0:T(8,128)(2,1)}), bf16[16,2,256,256]{3,2,1,0:T(8,128)(2,1)}) %all-gather.8.cloned.1.call-update) | async-done | bytes 4194320 | tf_op jit(solution)/shard_map/all_gather | solution.py:20
  90.8 2.6 %copy.16 = bf16[2,4,4,256,256]{4,3,2,1,0:T(8,128)(2,1)S(1)} copy(bf16[2,4,4,256,256]{4,3,0,1,2:T(8,128)(2,1)} %bitcast.68) | data formatting | bytes 8388608 | tf_op jit(solution)/shard_map/transpose | solution.py:23
  93.5 2.3 %fusion.45 = (bf16[8192,128]{1,0:T(8,128)(2,1)}, bf16[8192,128]{1,0:T(8,128)(2,1)}) fusion(bf16[8192,256]{1,0:T(8,128)(2,1)S(1)} %bitcast.65), kind=kLoop, calls=%fused_computation.42 | loop fusion | bytes 8388608 | tf_op jit(solution)/shard_map/slice | solution.py:52
  95.8 1.8 %copy-done = bf16[2,4,4,256,256]{4,3,2,1,0:T(8,128)(2,1)} copy-done((bf16[2,4,4,256,256]{4,3,2,1,0:T(8,128)(2,1)}, bf16[2,4,4,256,256]{4,3,2,1,0:T(8,128)(2,1)S(1)}, u32[]{:S(2)}) %copy-start) | copy-done | bytes 4194328
  97.6 1.2 slice-done.1
  98.8 1.2 fusion.6
  100.0 2.9 %copy.28 = bf16[8192,128]{0,1:T(8,128)(2,1)S(1)} copy(bf16[8192,128]{1,0:T(8,128)(2,1)} %get-tuple-element.5) | data formatting | bytes 4194304
  102.9 1.8 %neg.3 = bf16[8192,128]{0,1:T(8,128)(2,1)} negate(bf16[8192,128]{0,1:T(8,128)(2,1)S(1)} %copy.28) | non-fusion elementwise | flops 1048576 | bytes 4194304 | tf_op jit(solution)/shard_map/neg | solution.py:52
  104.7 2.9 %copy.29 = bf16[8192,128]{0,1:T(8,128)(2,1)S(1)} copy(bf16[8192,128]{1,0:T(8,128)(2,1)} %get-tuple-element.6) | data formatting | bytes 4194304
  107.6 7.1 %fusion.2 = f32[2,256,256]{2,1,0:T(8,128)S(1)} fusion(bf16[8192,256,1]{1,0,2:T(8,128)(2,1)} %bitcast.67, bf16[2,256,16384]{2,1,0:T(8,128)(2,1)} %param.6), kind=kOutput, calls=%fused_computation.2 | convolution fusion | flops 2147483648 | bytes 13107200 | tf_op jit(solution)/shard_map/frg,gc->frc/dot_general | solution.py:57
  114.7 3.5 %fusion.24 = f32[256,256]{1,0:T(8,128)S(1)} fusion(f32[256,256]{1,0:T(8,128)S(1)} %fusion.6, bf16[1,256,16384]{2,1,0:T(8,128)(2,1)} %param.7, bf16[8192,128]{0,1:T(8,128)(2,1)S(1)} %copy.29, bf16[8192,128]{0,1:T(8,128)(2,1)S(1)} %copy-done.1), kind=kOutput, calls=%fused_computation.17 | convolution fusion | flops 1082195968 | bytes 8912896 | tf_op jit(solution)/shard_map/frg,gc->frc/dot_general | solution.py:60
  118.2 5.8 %fusion.16 = f32[2,256,256]{2,1,0:T(8,128)S(1)} fusion(f32[2,256,256]{2,1,0:T(8,128)S(1)} %fusion.2, bf16[2,256,16384]{2,1,0:T(8,128)(2,1)} %param.6, bf16[8192,128]{0,1:T(8,128)(2,1)S(1)} %copy.29, bf16[8192,128]{0,1:T(8,128)(2,1)S(1)} %copy-done.1), kind=kOutput, calls=%fused_computation.14 | convolution fusion | flops 2156003328 | bytes 13631488 | tf_op jit(solution)/shard_map/frg,gc->frc/dot_general | solution.py:60
  124.0 0.6 convolution_bitcast_fusion
  124.7 0.4 convolution_bitcast_fusion.1
  125.1 0.3 fusion.30
  125.4 10.2 %all_to_all.10 = f32[4,32,256]{2,1,0:T(8,128)S(1)} all-to-all(f32[4,32,256]{2,1,0:T(8,128)S(1)} %fusion.30), channel_id=1, replica_groups=mesh['freq'=4,'gblk_0'=2,'gblk_1'=4,'gblk_2'=4] {'freq'}, dimensions={0} | all-to-all | bytes 262144 | tf_op jit(solution)/shard_map/all_to_all | solution.py:38
  135.6 14.4 %all_to_all.11 = f32[32,1,256]{2,1,0:T(1,128)S(1)} all-to-all(f32[32,1,256]{2,1,0:T(1,128)S(1)} %reshape.151), channel_id=1, replica_groups=mesh['freq'=4,'gblk_0'=2,'gblk_1'=4,'gblk_2'=4] {'gblk_0','gblk_1','gblk..., dimensions={0} | all-to-all | bytes 65536 | tf_op jit(solution)/shard_map/all_to_all | solution.py:38
  150.0 0.6 reduce_sum.38
  (18 shorter events, 0.1 us)
Async XLA Ops:
  6.5 34.2 %all-gather.6.cloned.1.call-start = ((), (), s32[]{:S(2)}) async-start(), calls=%async_computation.2 | async-start | bytes 1310720 | tf_op jit(solution)/shard_map/all_gather | solution.py:20
  14.2 76.7 %all-gather.8.cloned.1.call-start = ((), (), s32[]{:S(2)}) async-start(), calls=%async_computation.3 | async-start | bytes 5242880 | tf_op jit(solution)/shard_map/all_gather | solution.py:20
  90.8 6.7 %slice-start = ((s8[8388608]{0:T(1024)(128)(4,1)}), s8[4194304]{0:T(1024)(128)(4,1)S(1)}, s32[]{:S(2)}) async-start(s8[8388608]{0:T(1024)(128)(4,1)} %bitcast.71), calls=%async_computation.4 | async-start | bytes 8388608
  93.5 4.1 %copy-start = (bf16[2,4,4,256,256]{4,3,2,1,0:T(8,128)(2,1)}, bf16[2,4,4,256,256]{4,3,2,1,0:T(8,128)(2,1)S(1)}, u32[]{:S(2)}) copy-start(bf16[2,4,4,256,256]{4,3,2,1,0:T(8,128)(2,1)S(1)} %copy.16) | copy-start | bytes 12582916
  93.5 5.3 %slice-start.1 = ((s8[8388608]{0:T(1024)(128)(4,1)}), s8[4194304]{0:T(1024)(128)(4,1)S(1)}, s32[]{:S(2)}) async-start(s8[8388608]{0:T(1024)(128)(4,1)} %bitcast.71), calls=%async_computation.5 | async-start | bytes 8388608
  107.6 7.1 %copy-start.1 = (bf16[8192,128]{0,1:T(8,128)(2,1)S(1)}, bf16[8192,128]{0,1:T(8,128)(2,1)}, u32[]{:S(2)}) copy-start(bf16[8192,128]{0,1:T(8,128)(2,1)} %neg.3) | copy-start | bytes 6291460
  118.1 5.8 %copy-start.2 = (bf16[256,256]{1,0:T(8,128)(2,1)S(1)}, bf16[256,256]{1,0:T(8,128)(2,1)}, u32[]{:S(2)}) copy-start(bf16[256,256]{1,0:T(8,128)(2,1)} %param.8) | copy-start | bytes 393220
  118.2 6.9 %copy-start.3 = (f32[2,128]{1,0:T(2,128)S(1)}, f32[2,128]{1,0:T(2,128)}, u32[]{:S(2)}) copy-start(f32[2,128]{1,0:T(2,128)} %param.9) | copy-start | bytes 3076
Sparse Core Ops, SparseCore 0:
  14.3 26.3 all-gather.5
  42.4 48.3 all-gather.7
where the time goes:
time: 158 us; the launch traced here: 157 us
  waiting for transfers between devices  75.2 us (48%)
  blocking collectives  32.2 us (20%)
  matrix products  18.8 us (12%)
  local copies, waits for them, and re-layouts  14.5 us (9%)
  between operations  13.6 us (9%)
  other arithmetic  3.11 us (2%)
    all_gather x2, waiting for transfers between devices, all_blocks(): parts = lax.all_gather(parts, axes[k])  75.2 us
    all_to_all x2, blocking collectives, summed_on_arrival(): lax.all_to_all(parts, axis, split_axis=0, concat_axis=0, tiled=True)  24.6 us
    dot_general x2, matrix products, contrib(): jnp.einsum('frg,gc->frc', lower_cols, lower_rows, preferred_element_type=...  9.28 us
    unnamed x14, local copies, waits for them, and re-layouts  8.83 us
    dot_general x2, matrix products, contrib(): jnp.einsum('frg,gc->frc', upper_cols, shard_rows, preferred_element_type=...  8.29 us
    all_gather x1, blocking collectives, all_blocks(): parts = lax.all_gather(parts, axes[k])  7.61 us
  transfers between devices with their start and end apart: 2, of which 2 were waited for; matrix products, arithmetic and copies ran while one was open for 1% of the time, Pallas kernels for 0%

commit v1 on v0

v1 whole, which is shorter than its diff:
```python
import functools
import jax
import jax.numpy as jnp
from jax import lax
from jax.experimental import pallas as pl
from jax.experimental.pallas import tpu as pltpu
from jax.sharding import Mesh
from jax.sharding import PartitionSpec as P


NAMES = ("xh", "c", "xl", "z", "y")
PLANE = ("c", "xl", "z", "y")
ALL = NAMES
COLS = 1024
FIRST = 3
NEAR = (0, 1, 3, 2)
FAR = (0, 1, 3, 2)


def device_id(xl, c, z, y):
    return ((c * 2 + xl) * 4 + z % 4) * 4 + y % 4


def moved(x, target):
    pairs = []
    for xl in range(2):
        for c in range(2):
            for z in range(4):
                for y in range(4):
                    to = target(xl, c, z, y)
                    if to is not None:
                        pairs.append((device_id(xl, c, z, y), device_id(*to)))
    return lax.ppermute(x, PLANE, pairs)


def to_class_core(x, k):
    def target(xl, c, z, y):
        if c == xl and k == 0:
            return None
        at = xl if c == xl else 1 - xl
        return (at, xl, z, y + k) if xl == 0 else (at, xl, z + k, y)

    return moved(x, target)


def along_other(x, k):
    return moved(x, lambda xl, c, z, y: (xl, c, z + k, y) if c == 0 else (xl, c, z, y + k))


def other_core(x):
    return moved(x, lambda xl, c, z, y: (xl, 1 - c, z, y))


def prep_kernel(at_ref, m_ref, owner_ref, residue_ref, quad_ref, l_ref, q_ref):
    nb = owner_ref.shape[1]
    owner = jnp.broadcast_to(owner_ref[...].astype(jnp.float32), (nb, nb)).T
    lanes = lax.broadcasted_iota(jnp.int32, (nb, nb), 1)
    pick = (owner.astype(jnp.int32) == lanes).astype(jnp.float32)
    pick16 = pick.astype(jnp.bfloat16)
    nt = (((1,), (1,)), ((), ()))
    g = m_ref.shape[0]
    re = lax.dot_general(pick16, m_ref[:, :nb], nt, preferred_element_type=jnp.float32)
    im = lax.dot_general(pick16, m_ref[:, nb:], nt, preferred_element_type=jnp.float32)
    l_ref[:nb, :g] = re.astype(jnp.bfloat16)
    l_ref[:nb, g:] = im.astype(jnp.bfloat16)
    l_ref[nb:, :g] = (-im).astype(jnp.bfloat16)
    l_ref[nb:, g:] = re.astype(jnp.bfloat16)
    nq = quad_ref.shape[0]
    fid = at_ref[4]
    rows = [quad_ref[f : f + 1, :] for f in range(nq)]
    for r in range(q_ref.shape[0] - nq):
        rows.append((residue_ref[...] == fid + r).astype(jnp.float32))
    for f, row in enumerate(rows):
        weight = jnp.sum(pick * row, axis=1, keepdims=True)
        q_ref[f] = jnp.broadcast_to(weight, (nb, nb))


def prepare(at, m, owner, residue, quad, n_freq):
    g, width = m.shape
    nb = width // 2
    whole = lambda *shape: pl.BlockSpec(shape, lambda i: (0,) * len(shape))
    return pl.pallas_call(
        prep_kernel,
        grid=(1,),
        in_specs=[
            pl.BlockSpec(memory_space=pltpu.SMEM),
            whole(g, width),
            whole(1, nb),
            whole(1, nb),
            whole(*quad.shape),
        ],
        out_specs=[whole(2 * nb, 2 * g), whole(n_freq, nb, nb)],
        out_shape=[
            jax.ShapeDtypeStruct((2 * nb, 2 * g), jnp.bfloat16),
            jax.ShapeDtypeStruct((n_freq, nb, nb), jnp.float32),
        ],
        compiler_params=pltpu.CompilerParams(vmem_limit_bytes=8 * 2**20),
        name="prep",
    )(at, m, owner.reshape(1, -1), residue.reshape(1, -1), quad)


def left_kernel(l_ref, q_ref, wir_ref, wii_ref, wrr_ref, wri_ref, *rest, base, blk):
    z_ref = rest[-1]
    g = wir_ref.shape[1]
    nb = q_ref.shape[1]
    n = wir_ref.shape[2]
    total = None
    f = 0
    for re_ref, im_ref in ((wir_ref, wii_ref), (wrr_ref, wri_ref)):
        for k in range(re_ref.shape[0]):
            part = jnp.dot(l_ref[:, :g], re_ref[k], preferred_element_type=jnp.float32)
            part = part + jnp.dot(l_ref[:, g:], im_ref[k], preferred_element_type=jnp.float32)
            weight = jnp.concatenate([q_ref[f]] * (n // nb), axis=1)
            weight = jnp.concatenate([weight, weight], axis=0)
            total = part * weight if total is None else total + part * weight
            f += 1
    hi = total.astype(jnp.bfloat16)
    lo = (total - hi.astype(jnp.float32)).astype(jnp.bfloat16)
    at = (base + pl.program_id(0)) * (n // blk)
    for j in range(n // blk):
        z_ref[at + j, : 2 * nb, :] = hi[:, j * blk : (j + 1) * blk]
        z_ref[at + j, 2 * nb :, :] = lo[:, j * blk : (j + 1) * blk]


def left(l, q, w_imag, w_real, z, base, steps):
    fi, g, width = w_imag.shape
    fr = w_real.shape[0]
    nb = q.shape[1]
    blk = 256
    half = width // 2 // COLS
    re_map = lambda i: (0, 0, base + i)
    im_map = lambda i: (0, 0, base + half + i)
    in_specs = [
        pl.BlockSpec(memory_space=pltpu.VMEM),
        pl.BlockSpec(memory_space=pltpu.VMEM),
        pl.BlockSpec((fi, g, COLS), re_map),
        pl.BlockSpec((fi, g, COLS), im_map),
        pl.BlockSpec((fr, g, COLS), re_map),
        pl.BlockSpec((fr, g, COLS), im_map),
    ]
    args = [l, q, w_imag, w_imag, w_real, w_real]
    aliases = {}
    if z is not None:
        in_specs.append(pl.BlockSpec(memory_space=pltpu.VMEM))
        aliases = {len(args): 0}
        args.append(z)
    shape = (width // 2 // blk, 4 * nb, blk)
    flops = 2 * (fi + fr) * 2 * nb * 2 * g * COLS * steps
    return pl.pallas_call(
        functools.partial(left_kernel, base=base, blk=blk),
        grid=(steps,),
        in_specs=in_specs,
        out_specs=pl.BlockSpec(memory_space=pltpu.VMEM),
        out_shape=pltpu.VMEM(shape, jnp.bfloat16),
        input_output_aliases=aliases,
        cost_estimate=pl.CostEstimate(
            flops=flops, bytes_accessed=2 * (fi + fr) * g * 2 * COLS * steps, transcendentals=0
        ),
        compiler_params=pltpu.CompilerParams(vmem_limit_bytes=32 * 2**20),
    )(*args)


def right_kernel(at_ref, z_ref, *refs, slots, final, seeded):
    refs = list(refs)
    out_ref = refs.pop()
    total = refs.pop(0)[...] if seeded else None
    c, z, y = at_ref[0], at_ref[2], at_ref[3]
    for m_ref, (swapped, far) in zip(refs, slots):
        cls = 1 - c if swapped else c
        for j in range(m_ref.shape[0]):
            near = NEAR[j]
            dz = jnp.where(cls == 0, far, near)
            dy = jnp.where(cls == 0, near, far)
            block = cls * 16 + lax.rem(z - dz + 4, 4) * 4 + lax.rem(y - dy + 4, 4)
            part = jnp.dot(z_ref[block], m_ref[j], preferred_element_type=jnp.float32)
            total = part if total is None else total + part
    if final:
        rows = total.shape[0] // 2
        both = total[:rows] + total[rows:]
        nb = rows // 2
        out_ref[:, :nb] = both[:nb, :nb] - both[nb:, nb:]
        out_ref[:, nb:] = both[:nb, nb:] + both[nb:, :nb]
    else:
        out_ref[...] = total


def stack_kernel(at_ref, own_ref, first_ref, *refs):
    out_ref = refs[-1]
    mine = at_ref[0] == at_ref[1]

    @pl.when(mine)
    def _():
        out_ref[0] = own_ref[...]

    @pl.when(jnp.logical_not(mine))
    def _():
        out_ref[0] = first_ref[...]

    for k, ref in enumerate(refs[:-1]):
        out_ref[k + 1] = ref[...]


def stack(at, own, near):
    return pl.pallas_call(
        stack_kernel,
        in_specs=[pl.BlockSpec(memory_space=pltpu.SMEM)]
        + [pl.BlockSpec(memory_space=pltpu.VMEM) for _ in range(1 + len(near))],
        out_specs=pl.BlockSpec(memory_space=pltpu.VMEM),
        out_shape=jax.ShapeDtypeStruct((len(near),) + own.shape, own.dtype),
        compiler_params=pltpu.CompilerParams(vmem_limit_bytes=4 * 2**20),
        name="stack",
    )(at, own, *near)


def right(at, z, pieces, slots, seed, final):
    rows = z.shape[1]
    shape = (rows // 4, z.shape[2]) if final else (rows, z.shape[2])
    args = [at, z] + ([seed] if seed is not None else []) + list(pieces)
    blocks = sum(p.shape[0] for p in pieces)
    return pl.pallas_call(
        functools.partial(right_kernel, slots=slots, final=final, seeded=seed is not None),
        in_specs=[pl.BlockSpec(memory_space=pltpu.SMEM)]
        + [pl.BlockSpec(memory_space=pltpu.VMEM) for _ in args[1:]],
        out_specs=pl.BlockSpec(memory_space=pltpu.VMEM),
        out_shape=jax.ShapeDtypeStruct(shape, jnp.float32),
        cost_estimate=pl.CostEstimate(
            flops=2 * rows * 256 * 256 * blocks, bytes_accessed=0, transcendentals=0
        ),
        compiler_params=pltpu.CompilerParams(vmem_limit_bytes=24 * 2**20),
        name="right_last" if final else "right_first",
    )(*args)


def on_device(w_imag, w_real, pair_elements, quad_weight, residue_freq, owner_bands):
    bands = pair_elements.shape[1] // 2
    c, xl, z, y = (lax.axis_index(a) for a in ("c", "xl", "z", "y"))
    fid = lax.axis_index(("xh", "c")) * w_real.shape[0]
    at = jnp.stack([c, xl, z, y, fid]).astype(jnp.int32)
    n_freq = w_imag.shape[0] + w_real.shape[0]

    w_real = pltpu.with_memory_space_constraint(w_real, pltpu.HBM)
    w_imag = pltpu.with_memory_space_constraint(w_imag, pltpu.HBM)
    near = []
    for k in NEAR:
        near.append(to_class_core(pair_elements, k))
    l, q = prepare(
        at,
        pair_elements,
        owner_bands,
        residue_freq,
        quad_weight,
        n_freq,
    )
    zl = left(l, q, w_imag, w_real, None, 0, FIRST)
    four = stack(at, pair_elements, near)
    far = []
    for k in FAR[1:]:
        far.append(along_other(four, k))
    zl = left(l, q, w_imag, w_real, zl, FIRST, 8 - FIRST)
    mine = [four] + far
    theirs = []
    for p in mine:
        theirs.append(other_core(p))

    slots = [(s, f) for s in (False, True) for f in FAR]
    first = right(at, zl, mine[:3] + theirs[:3], slots[:3] + slots[4:7], None, False)
    total = right(at, zl, [mine[3], theirs[3]], [slots[3], slots[7]], first, True)

    n_dev = 128
    parts = total.reshape(n_dev, 1, 2 * bands)
    arrived = lax.all_to_all(parts, ALL, split_axis=0, concat_axis=0, tiled=True)
    return arrived.sum(axis=0)


def solution(mesh):
    torus = Mesh(mesh.devices.reshape(2, 2, 2, 4, 4), NAMES)
    freq, gblk = ("xh", "c"), ("xl", "z", "y")
    placed = (
        P(freq, gblk, None),
        P(freq, gblk, None),
        P(gblk, None),
        P(freq, None),
        P(),
        P(),
    )
    return jax.shard_map(
        on_device, mesh=torus, in_specs=placed, out_specs=P(NAMES, None), check_vma=False
    )
```

time: 158 us -> 73.3 us (0.46)
  waiting for transfers between devices: 75.2 us -> 5.96 us
  starting transfers between devices: 0.04 us -> 21.1 us
  Pallas kernels: 0 us -> 19.7 us
  matrix products: 18.8 us -> 0 us
  between operations: 13.6 us -> 0.12 us
  blocking collectives: 32.2 us -> 20.9 us
  local copies, waits for them, and re-layouts: 14.5 us -> 4.02 us
  other arithmetic: 3.11 us -> 0.71 us
    all_gather x2 -> x0, waiting for transfers between devices: 75.2 us -> none  [all_blocks(): parts = lax.all_gather(parts, axes[k])]
    ppermute x0 -> x11, starting transfers between devices: none -> 21.1 us  [moved(): return lax.ppermute(x, PLANE, pairs)]
    pallas_call x0 -> x6, Pallas kernels: none -> 19.7 us  [the longest x2 14.7 us: left(): pl.pallas_call(functools.partial(left_kernel, base=base, blk=blk), grid=(...]
    dot_general x7 -> x0, matrix products: 18.8 us -> none  [the longest x2 9.28 us: contrib(): jnp.einsum('frg,gc->frc', lower_cols, lower_rows, preferred_element_type=...]
    all_gather x1 -> x0, blocking collectives: 7.61 us -> none  [all_blocks(): parts = lax.all_gather(parts, axes[k])]
    ppermute x0 -> x11, waiting for transfers between devices: none -> 5.96 us  [moved(): return lax.ppermute(x, PLANE, pairs)]
    unnamed x14 -> x10, local copies, waits for them, and re-layouts: 8.83 us -> 3.8 us
    all_to_all x2 -> x1, blocking collectives: 24.6 us -> 20.9 us  [on_device(): lax.all_to_all(parts, ALL, split_axis=0, concat_axis=0, tiled=True)]
  transfers between devices with their start and end apart: 2 -> 11, of which waited for: 2 -> 4; matrix products, arithmetic and copies ran while one was open for 1% -> 0% of each run, Pallas kernels for 0% -> 25%
where the time goes in v1:
time: 73.3 us; the launch traced here: 72.4 us
  starting transfers between devices  21.1 us (29%)
  blocking collectives  20.9 us (29%)
  Pallas kernels  19.7 us (27%)
  waiting for transfers between devices  5.96 us (8%)
  local copies, waits for them, and re-layouts  4.02 us (5%)
    ppermute x11, starting transfers between devices, moved(): return lax.ppermute(x, PLANE, pairs)  21.1 us
    all_to_all x1, blocking collectives, on_device(): lax.all_to_all(parts, ALL, split_axis=0, concat_axis=0, tiled=True)  20.9 us
    pallas_call x2, Pallas kernels, left(): pl.pallas_call(functools.partial(left_kernel, base=base, blk=blk), grid=(...  14.7 us
    ppermute x11, waiting for transfers between devices, moved(): return lax.ppermute(x, PLANE, pairs)  5.96 us
    unnamed x10, local copies, waits for them, and re-layouts  3.8 us
    pallas_call x2, Pallas kernels, right(): pl.pallas_call(functools.partial(right_kernel, slots=slots, final=final,...  3.6 us
  transfers between devices with their start and end apart: 11, of which 4 were waited for; matrix products, arithmetic and copies ran while one was open for 0% of the time, Pallas kernels for 25%

profile of v1, /device:TPU:0, one launch (start us, length us, event | category | flops | bytes accessed | tf_op | source)
XLA Modules:
  0.0 72.4 jit_solution(15768469815994205164)
XLA Ops:
  0.0 0.7 collective-permute-start
  0.7 1.8 %collective-permute-start.1 = (bf16[256,256]{1,0:T(8,128)(2,1)}, bf16[256,256]{1,0:T(8,128)(2,1)S(1)}, u32[]{:S(2)}, u32[]{:S(2)}) collective-permute-start(bf16[256,256]{1,0:T(8,128)(2,1)} %own_ref.1), channel_id=1, source_target_pairs={{0,1},{1,2},{2,3},{3,0},{4,5},{5,6},{6,7},{7,4},{8,9},{9,10},{10,1... | collective-permute-start | bytes 393224 | tf_op jit(solution)/shard_map/ppermute | solution.py:33
  2.4 1.5 %collective-permute-start.2 = (bf16[256,256]{1,0:T(8,128)(2,1)}, bf16[256,256]{1,0:T(8,128)(2,1)S(1)}, u32[]{:S(2)}, u32[]{:S(2)}) collective-permute-start(bf16[256,256]{1,0:T(8,128)(2,1)} %own_ref.1), channel_id=1, source_target_pairs={{0,3},{1,0},{2,1},{3,2},{4,7},{5,4},{6,5},{7,6},{8,11},{9,8},{10,9... | collective-permute-start | bytes 393224 | tf_op jit(solution)/shard_map/ppermute | solution.py:33
  4.0 2.1 %collective-permute-start.3 = (bf16[256,256]{1,0:T(8,128)(2,1)}, bf16[256,256]{1,0:T(8,128)(2,1)S(1)}, u32[]{:S(2)}, u32[]{:S(2)}) collective-permute-start(bf16[256,256]{1,0:T(8,128)(2,1)} %own_ref.1), channel_id=1, source_target_pairs={{0,2},{1,3},{2,0},{3,1},{4,6},{5,7},{6,4},{7,5},{8,10},{9,11},{10,... | collective-permute-start | bytes 393224 | tf_op jit(solution)/shard_map/ppermute | solution.py:33
  6.2 1.0 %collective-permute-done.1.refs_0_ = bf16[256,256]{1,0:T(8,128)(2,1)S(1)} collective-permute-done((bf16[256,256]{1,0:T(8,128)(2,1)}, bf16[256,256]{1,0:T(8,128)(2,1)S(1)}, u32[]{:S(2)}, u32[]{:S(2)}) %collective-permute-start.1) | collective-permute-done | bytes 131104 | tf_op jit(solution)/shard_map/ppermute | solution.py:33
  7.6 3.1 %collective-permute-done.3.refs_2_ = bf16[256,256]{1,0:T(8,128)(2,1)S(1)} collective-permute-done((bf16[256,256]{1,0:T(8,128)(2,1)}, bf16[256,256]{1,0:T(8,128)(2,1)S(1)}, u32[]{:S(2)}, u32[]{:S(2)}) %collective-permute-start.3) | collective-permute-done | bytes 131104 | tf_op jit(solution)/shard_map/ppermute | solution.py:33
  10.7 0.9 %copy-done = bf16[256,256]{1,0:T(8,128)(2,1)S(1)} copy-done((bf16[256,256]{1,0:T(8,128)(2,1)S(1)}, bf16[256,256]{1,0:T(8,128)(2,1)}, u32[]{:S(2)}) %copy-start) | copy-done | bytes 131096
  12.2 2.1 %collective-permute-start.4 = (bf16[4,256,256]{2,1,0:T(8,128)(2,1)S(1)}, bf16[4,256,256]{2,1,0:T(8,128)(2,1)S(1)}, u32[]{:S(2)}, u32[]{:S(2)}) collective-permute-start(bf16[4,256,256]{2,1,0:T(8,128)(2,1)S(1)} %stack.25.refs_0_), channel_id=1, source_target_pairs={{0,4},{1,5},{2,6},{3,7},{4,8},{5,9},{6,10},{7,11},{8,12},{9,13},{1... | collective-permute-start | bytes 1572872 | tf_op jit(solution)/shard_map/ppermute | solution.py:33
  14.2 2.2 %collective-permute-start.5 = (bf16[4,256,256]{2,1,0:T(8,128)(2,1)S(1)}, bf16[4,256,256]{2,1,0:T(8,128)(2,1)S(1)}, u32[]{:S(2)}, u32[]{:S(2)}) collective-permute-start(bf16[4,256,256]{2,1,0:T(8,128)(2,1)S(1)} %stack.25.refs_0_), channel_id=1, source_target_pairs={{0,12},{1,13},{2,14},{3,15},{4,0},{5,1},{6,2},{7,3},{8,4},{9,5},{1... | collective-permute-start | bytes 1572872 | tf_op jit(solution)/shard_map/ppermute | solution.py:33
  16.5 1.8 %collective-permute-start.9 = (bf16[4,256,256]{2,1,0:T(8,128)(2,1)S(1)}, bf16[4,256,256]{2,1,0:T(8,128)(2,1)S(1)}, u32[]{:S(2)}, u32[]{:S(2)}) collective-permute-start(bf16[4,256,256]{2,1,0:T(8,128)(2,1)S(1)} %stack.25.refs_0_), channel_id=1, source_target_pairs={{0,8},{1,9},{2,10},{3,11},{4,12},{5,13},{6,14},{7,15},{8,0},{9,1},... | collective-permute-start | bytes 1572872 | tf_op jit(solution)/shard_map/ppermute | solution.py:33
  18.2 0.9 %copy-done.1 = bf16[256,256]{1,0:T(8,128)(2,1)S(1)} copy-done((bf16[256,256]{1,0:T(8,128)(2,1)S(1)}, bf16[256,256]{1,0:T(8,128)(2,1)}, u32[]{:S(2)}) %copy-start.1) | copy-done | bytes 131096
  19.1 0.7 copy-done.2
  19.8 0.7 copy-done.3
  21.1 0.8 %prep.1 = (bf16[256,512]{1,0:T(8,128)(2,1)S(1)}, f32[3,128,128]{2,1,0:T(8,128)S(1)}) custom-call(s32[5]{0:T(128)S(1)} %stack.24.at_ref, bf16[256,256]{1,0:T(8,128)(2,1)S(1)} %copy-done.1, s32[1,128]{1,0:T(1,128)S(1)} %bitcast.10, s32[1,128]{1,0:T(1,128)S(1)} %bitcast.11, f32[2,128]{1,0:T(2,128)S(1)} %copy-done.2), custom_call_target="tpu_custom_call" | custom-call | tf_op jit(solution)/shard_map/prep/pallas_call | solution.py:82
  21.9 3.3 %collective-permute-start.6 = (bf16[4,256,256]{2,1,0:T(8,128)(2,1)S(1)}, bf16[4,256,256]{2,1,0:T(8,128)(2,1)S(1)}, u32[]{:S(2)}, u32[]{:S(2)}) collective-permute-start(bf16[4,256,256]{2,1,0:T(8,128)(2,1)S(1)} %stack.25.refs_0_), channel_id=1, source_target_pairs={{0,32},{1,33},{2,34},{3,35},{4,36},{5,37},{6,38},{7,39},{8,40},{9,... | collective-permute-start | bytes 1572872 | tf_op jit(solution)/shard_map/ppermute | solution.py:33
  25.2 2.2 %collective-permute-start.7 = (bf16[4,256,256]{2,1,0:T(8,128)(2,1)S(1)}, bf16[4,256,256]{2,1,0:T(8,128)(2,1)S(1)}, u32[]{:S(2)}, u32[]{:S(2)}) collective-permute-start(bf16[4,256,256]{2,1,0:T(8,128)(2,1)S(1)} %collective-permute-done.4.refs_1_), channel_id=1, source_target_pairs={{0,32},{1,33},{2,34},{3,35},{4,36},{5,37},{6,38},{7,39},{8,40},{9,... | collective-permute-start | bytes 1572872 | tf_op jit(solution)/shard_map/ppermute | solution.py:33
  27.4 1.4 %collective-permute-done.5.refs_2_ = bf16[4,256,256]{2,1,0:T(8,128)(2,1)S(1)} collective-permute-done((bf16[4,256,256]{2,1,0:T(8,128)(2,1)S(1)}, bf16[4,256,256]{2,1,0:T(8,128)(2,1)S(1)}, u32[]{:S(2)}, u32[]{:S(2)}) %collective-permute-start.5) | collective-permute-done | bytes 524320 | tf_op jit(solution)/shard_map/ppermute | solution.py:33
  28.8 3.4 %collective-permute-start.8 = (bf16[4,256,256]{2,1,0:T(8,128)(2,1)S(1)}, bf16[4,256,256]{2,1,0:T(8,128)(2,1)S(1)}, u32[]{:S(2)}, u32[]{:S(2)}) collective-permute-start(bf16[4,256,256]{2,1,0:T(8,128)(2,1)S(1)} %collective-permute-done.5.refs_2_), channel_id=1, source_target_pairs={{0,32},{1,33},{2,34},{3,35},{4,36},{5,37},{6,38},{7,39},{8,40},{9,... | collective-permute-start | bytes 1572872 | tf_op jit(solution)/shard_map/ppermute | solution.py:33
  32.2 5.9 %shard_map.64.rest_0_ = bf16[32,512,256]{2,1,0:T(8,128)(2,1)S(1)} custom-call(bf16[256,512]{1,0:T(8,128)(2,1)S(1)} %get-tuple-element.7.l_ref, f32[3,128,128]{2,1,0:T(8,128)S(1)} %get-tuple-element.8.q_ref, bf16[2,256,16384]{2,1,0:T(8,128)(2,1)} %wii_ref.3, bf16[2,256,16384]{2,1,0:T(8,128)(2,1)} %wii_ref.3, bf16[1,256,16384]{2,1,0:T(8,128)(2,1)} %wri_ref.3, ...), custom_call_target="tpu_custom_call" | custom-call | flops 2415919104 | bytes 9437184 | tf_op jit(solution)/shard_map/pallas_call | solution.py:149
  38.2 8.8 %shard_map.65.z_ref = bf16[32,512,256]{2,1,0:T(8,128)(2,1)S(1)} custom-call(bf16[256,512]{1,0:T(8,128)(2,1)S(1)} %get-tuple-element.7.l_ref, f32[3,128,128]{2,1,0:T(8,128)S(1)} %get-tuple-element.8.q_ref, bf16[2,256,16384]{2,1,0:T(8,128)(2,1)} %wii_ref.3, bf16[2,256,16384]{2,1,0:T(8,128)(2,1)} %wii_ref.3, ...), custom_call_target="tpu_custom_call", output_to_operand_aliasing={{}: (6, {})} | custom-call | flops 4026531840 | bytes 15728640 | tf_op jit(solution)/shard_map/pallas_call | solution.py:149
  47.1 2.3 %right_first.1.refs_0_ = f32[512,256]{1,0:T(8,128)S(1)} custom-call(s32[5]{0:T(128)S(1)} %stack.24.at_ref, bf16[32,512,256]{2,1,0:T(8,128)(2,1)S(1)} %shard_map.65.z_ref, bf16[4,256,256]{2,1,0:T(8,128)(2,1)S(1)} %stack.25.refs_0_, bf16[4,256,256]{2,1,0:T(8,128)(2,1)S(1)} %collective-permute-done.4.refs_1_, ...), custom_call_target="tpu_custom_call" | custom-call | flops 1610612736 | tf_op jit(solution)/shard_map/right_first/pallas_call | solution.py:220
  49.4 1.3 %right_last.1 = f32[128,256]{1,0:T(8,128)S(1)} custom-call(s32[5]{0:T(128)S(1)} %stack.24.at_ref, bf16[32,512,256]{2,1,0:T(8,128)(2,1)S(1)} %shard_map.65.z_ref, f32[512,256]{1,0:T(8,128)S(1)} %right_first.1.refs_0_, bf16[4,256,256]{2,1,0:T(8,128)(2,1)S(1)} %collective-permute-done.9.refs_1_, bf16[4,256,256]{2,1,0:T(8,128)(2,1)S(1)} %collective-permute-done.10.refs_2_), custom_call_target="tpu_custom_call" | custom-call | flops 536870912 | tf_op jit(solution)/shard_map/right_last/pallas_call | solution.py:220
  50.9 20.9 %all_to_all.5 = f32[128,1,256]{2,1,0:T(1,128)S(1)} all-to-all(f32[128,1,256]{2,1,0:T(1,128)S(1)} %copy.8), channel_id=1, replica_groups=mesh['xh'=2,'c'=2,'xl'=2,'z'=4,'y'=4] {'xh','c','xl','z','y'}, dimensions={0} | all-to-all | bytes 262144 | tf_op jit(solution)/shard_map/all_to_all | solution.py:271
  71.7 0.7 reduce_sum.11
  (18 shorter events, 2.0 us)
Async XLA Ops:
  0.0 6.2 %collective-permute-start = (bf16[256,256]{1,0:T(8,128)(2,1)}, bf16[256,256]{1,0:T(8,128)(2,1)S(1)}, u32[]{:S(2)}, u32[]{:S(2)}) collective-permute-start(bf16[256,256]{1,0:T(8,128)(2,1)} %own_ref.1), channel_id=1, source_target_pairs={{32,16},{33,17},{34,18},{35,19},{36,20},{37,21},{38,22},{39,23},{4... | collective-permute-start | bytes 393224 | tf_op jit(solution)/shard_map/ppermute | solution.py:33
  0.7 6.5 %collective-permute-start.1 = (bf16[256,256]{1,0:T(8,128)(2,1)}, bf16[256,256]{1,0:T(8,128)(2,1)S(1)}, u32[]{:S(2)}, u32[]{:S(2)}) collective-permute-start(bf16[256,256]{1,0:T(8,128)(2,1)} %own_ref.1), channel_id=1, source_target_pairs={{0,1},{1,2},{2,3},{3,0},{4,5},{5,6},{6,7},{7,4},{8,9},{9,10},{10,1... | collective-permute-start | bytes 393224 | tf_op jit(solution)/shard_map/ppermute | solution.py:33
  2.4 5.2 %collective-permute-start.2 = (bf16[256,256]{1,0:T(8,128)(2,1)}, bf16[256,256]{1,0:T(8,128)(2,1)S(1)}, u32[]{:S(2)}, u32[]{:S(2)}) collective-permute-start(bf16[256,256]{1,0:T(8,128)(2,1)} %own_ref.1), channel_id=1, source_target_pairs={{0,3},{1,0},{2,1},{3,2},{4,7},{5,4},{6,5},{7,6},{8,11},{9,8},{10,9... | collective-permute-start | bytes 393224 | tf_op jit(solution)/shard_map/ppermute | solution.py:33
  4.0 6.7 %collective-permute-start.3 = (bf16[256,256]{1,0:T(8,128)(2,1)}, bf16[256,256]{1,0:T(8,128)(2,1)S(1)}, u32[]{:S(2)}, u32[]{:S(2)}) collective-permute-start(bf16[256,256]{1,0:T(8,128)(2,1)} %own_ref.1), channel_id=1, source_target_pairs={{0,2},{1,3},{2,0},{3,1},{4,6},{5,7},{6,4},{7,5},{8,10},{9,11},{10,... | collective-permute-start | bytes 393224 | tf_op jit(solution)/shard_map/ppermute | solution.py:33
  10.7 0.9 %copy-start = (bf16[256,256]{1,0:T(8,128)(2,1)S(1)}, bf16[256,256]{1,0:T(8,128)(2,1)}, u32[]{:S(2)}) copy-start(bf16[256,256]{1,0:T(8,128)(2,1)} %own_ref.1) | copy-start | bytes 393220
  12.2 13.0 %collective-permute-start.4 = (bf16[4,256,256]{2,1,0:T(8,128)(2,1)S(1)}, bf16[4,256,256]{2,1,0:T(8,128)(2,1)S(1)}, u32[]{:S(2)}, u32[]{:S(2)}) collective-permute-start(bf16[4,256,256]{2,1,0:T(8,128)(2,1)S(1)} %stack.25.refs_0_), channel_id=1, source_target_pairs={{0,4},{1,5},{2,6},{3,7},{4,8},{5,9},{6,10},{7,11},{8,12},{9,13},{1... | collective-permute-start | bytes 1572872 | tf_op jit(solution)/shard_map/ppermute | solution.py:33
  14.2 14.6 %collective-permute-start.5 = (bf16[4,256,256]{2,1,0:T(8,128)(2,1)S(1)}, bf16[4,256,256]{2,1,0:T(8,128)(2,1)S(1)}, u32[]{:S(2)}, u32[]{:S(2)}) collective-permute-start(bf16[4,256,256]{2,1,0:T(8,128)(2,1)S(1)} %stack.25.refs_0_), channel_id=1, source_target_pairs={{0,12},{1,13},{2,14},{3,15},{4,0},{5,1},{6,2},{7,3},{8,4},{9,5},{1... | collective-permute-start | bytes 1572872 | tf_op jit(solution)/shard_map/ppermute | solution.py:33
  16.5 21.7 %collective-permute-start.9 = (bf16[4,256,256]{2,1,0:T(8,128)(2,1)S(1)}, bf16[4,256,256]{2,1,0:T(8,128)(2,1)S(1)}, u32[]{:S(2)}, u32[]{:S(2)}) collective-permute-start(bf16[4,256,256]{2,1,0:T(8,128)(2,1)S(1)} %stack.25.refs_0_), channel_id=1, source_target_pairs={{0,8},{1,9},{2,10},{3,11},{4,12},{5,13},{6,14},{7,15},{8,0},{9,1},... | collective-permute-start | bytes 1572872 | tf_op jit(solution)/shard_map/ppermute | solution.py:33
  18.2 0.9 %copy-start.1 = (bf16[256,256]{1,0:T(8,128)(2,1)S(1)}, bf16[256,256]{1,0:T(8,128)(2,1)}, u32[]{:S(2)}) copy-start(bf16[256,256]{1,0:T(8,128)(2,1)} %own_ref.1) | copy-start | bytes 393220
  19.1 0.7 copy-start.2
  19.8 0.7 copy-start.3
  20.5 0.7 copy-start.4
  21.9 25.1 %collective-permute-start.6 = (bf16[4,256,256]{2,1,0:T(8,128)(2,1)S(1)}, bf16[4,256,256]{2,1,0:T(8,128)(2,1)S(1)}, u32[]{:S(2)}, u32[]{:S(2)}) collective-permute-start(bf16[4,256,256]{2,1,0:T(8,128)(2,1)S(1)} %stack.25.refs_0_), channel_id=1, source_target_pairs={{0,32},{1,33},{2,34},{3,35},{4,36},{5,37},{6,38},{7,39},{8,40},{9,... | collective-permute-start | bytes 1572872 | tf_op jit(solution)/shard_map/ppermute | solution.py:33
  25.2 21.9 %collective-permute-start.7 = (bf16[4,256,256]{2,1,0:T(8,128)(2,1)S(1)}, bf16[4,256,256]{2,1,0:T(8,128)(2,1)S(1)}, u32[]{:S(2)}, u32[]{:S(2)}) collective-permute-start(bf16[4,256,256]{2,1,0:T(8,128)(2,1)S(1)} %collective-permute-done.4.refs_1_), channel_id=1, source_target_pairs={{0,32},{1,33},{2,34},{3,35},{4,36},{5,37},{6,38},{7,39},{8,40},{9,... | collective-permute-start | bytes 1572872 | tf_op jit(solution)/shard_map/ppermute | solution.py:33
  28.8 18.3 %collective-permute-start.8 = (bf16[4,256,256]{2,1,0:T(8,128)(2,1)S(1)}, bf16[4,256,256]{2,1,0:T(8,128)(2,1)S(1)}, u32[]{:S(2)}, u32[]{:S(2)}) collective-permute-start(bf16[4,256,256]{2,1,0:T(8,128)(2,1)S(1)} %collective-permute-done.5.refs_2_), channel_id=1, source_target_pairs={{0,32},{1,33},{2,34},{3,35},{4,36},{5,37},{6,38},{7,39},{8,40},{9,... | collective-permute-start | bytes 1572872 | tf_op jit(solution)/shard_map/ppermute | solution.py:33
  38.1 11.3 %collective-permute-start.10 = (bf16[4,256,256]{2,1,0:T(8,128)(2,1)S(1)}, bf16[4,256,256]{2,1,0:T(8,128)(2,1)S(1)}, u32[]{:S(2)}, u32[]{:S(2)}) collective-permute-start(bf16[4,256,256]{2,1,0:T(8,128)(2,1)S(1)} %collective-permute-done.9.refs_1_), channel_id=1, source_target_pairs={{0,32},{1,33},{2,34},{3,35},{4,36},{5,37},{6,38},{7,39},{8,40},{9,... | collective-permute-start | bytes 1572872 | tf_op jit(solution)/shard_map/ppermute | solution.py:33

commit v2 on v1

--- a/solution.py
+++ b/solution.py
@@ -12,9 +12,9 @@
 PLANE = ("c", "xl", "z", "y")
 ALL = NAMES
 COLS = 1024
-FIRST = 3
+FIRST = 1
 NEAR = (0, 1, 3, 2)
-FAR = (0, 1, 3, 2)
+FAR = (0, 2, 1, 3)
 
 
 def device_id(xl, c, z, y):
@@ -96,74 +96,103 @@
         ],
         compiler_params=pltpu.CompilerParams(vmem_limit_bytes=8 * 2**20),
         name="prep",
-    )(at, m, owner.reshape(1, -1), residue.reshape(1, -1), quad)
-
-
-def left_kernel(l_ref, q_ref, wir_ref, wii_ref, wrr_ref, wri_ref, *rest, base, blk):
-    z_ref = rest[-1]
-    g = wir_ref.shape[1]
+    )(at, m, owner, residue, quad)
+
+
+def left_kernel(l_ref, q_ref, wi_ref, wr_ref, *rest, first, chunks):
+    z_ref, wi_buf, wr_buf, sem = rest[-4:]
+    g, width = wi_ref.shape[1:]
+    half = width // 2
     nb = q_ref.shape[1]
-    n = wir_ref.shape[2]
-    total = None
-    f = 0
-    for re_ref, im_ref in ((wir_ref, wii_ref), (wrr_ref, wri_ref)):
-        for k in range(re_ref.shape[0]):
-            part = jnp.dot(l_ref[:, :g], re_ref[k], preferred_element_type=jnp.float32)
-            part = part + jnp.dot(l_ref[:, g:], im_ref[k], preferred_element_type=jnp.float32)
-            weight = jnp.concatenate([q_ref[f]] * (n // nb), axis=1)
-            weight = jnp.concatenate([weight, weight], axis=0)
-            total = part * weight if total is None else total + part * weight
-            f += 1
-    hi = total.astype(jnp.bfloat16)
-    lo = (total - hi.astype(jnp.float32)).astype(jnp.bfloat16)
-    at = (base + pl.program_id(0)) * (n // blk)
-    for j in range(n // blk):
-        z_ref[at + j, : 2 * nb, :] = hi[:, j * blk : (j + 1) * blk]
-        z_ref[at + j, 2 * nb :, :] = lo[:, j * blk : (j + 1) * blk]
-
-
-def left(l, q, w_imag, w_real, z, base, steps):
+    blk = z_ref.shape[2]
+
+    def copies(j):
+        col = (first + j) * COLS
+        out = []
+        for part in range(2):
+            for k, (src, buf) in enumerate(((wi_ref, wi_buf), (wr_ref, wr_buf))):
+                cols = pl.ds(part * half + col, COLS)
+                out.append(
+                    pltpu.make_async_copy(
+                        src.at[:, :, cols], buf.at[j, part], sem.at[j, 2 * part + k]
+                    )
+                )
+        return out
+
+    for j in range(chunks):
+        for copy in copies(j):
+            copy.start()
+
+    for j in range(chunks):
+        for copy in copies(j):
+            copy.wait()
+        for s in range(COLS // blk):
+            cols = pl.ds(s * blk, blk)
+            total = None
+            f = 0
+            for buf in (wi_buf, wr_buf):
+                for k in range(buf.shape[2]):
+                    part = jnp.dot(
+                        l_ref[:, :g], buf[j, 0, k, :, cols], preferred_element_type=jnp.float32
+                    )
+                    part = part + jnp.dot(
+                        l_ref[:, g:], buf[j, 1, k, :, cols], preferred_element_type=jnp.float32
+                    )
+                    weight = jnp.concatenate([q_ref[f]] * (blk // nb), axis=1)
+                    weight = jnp.concatenate([weight, weight], axis=0)
+                    total = part * weight if total is None else total + part * weight
+                    f += 1
+            hi = total.astype(jnp.bfloat16)
+            lo = (total - hi.astype(jnp.float32)).astype(jnp.bfloat16)
+            at = (first + j) * (COLS // blk) + s
+            z_ref[at, : 2 * nb, :] = hi
+            z_ref[at, 2 * nb :, :] = lo
+
+
+def left(l, q, w_imag, w_real, z, first, chunks):
     fi, g, width = w_imag.shape
     fr = w_real.shape[0]
     nb = q.shape[1]
-    blk = 256
-    half = width // 2 // COLS
-    re_map = lambda i: (0, 0, base + i)
-    im_map = lambda i: (0, 0, base + half + i)
+    blk = 2 * nb
     in_specs = [
         pl.BlockSpec(memory_space=pltpu.VMEM),
         pl.BlockSpec(memory_space=pltpu.VMEM),
-        pl.BlockSpec((fi, g, COLS), re_map),
-        pl.BlockSpec((fi, g, COLS), im_map),
-        pl.BlockSpec((fr, g, COLS), re_map),
-        pl.BlockSpec((fr, g, COLS), im_map),
+        pl.BlockSpec(memory_space=pltpu.HBM),
+        pl.BlockSpec(memory_space=pltpu.HBM),
     ]
-    args = [l, q, w_imag, w_imag, w_real, w_real]
+    args = [l, q, w_imag, w_real]
     aliases = {}
     if z is not None:
         in_specs.append(pl.BlockSpec(memory_space=pltpu.VMEM))
         aliases = {len(args): 0}
         args.append(z)
     shape = (width // 2 // blk, 4 * nb, blk)
-    flops = 2 * (fi + fr) * 2 * nb * 2 * g * COLS * steps
+    flops = 2 * (fi + fr) * 2 * nb * 2 * g * COLS * chunks
     return pl.pallas_call(
-        functools.partial(left_kernel, base=base, blk=blk),
-        grid=(steps,),
+        functools.partial(left_kernel, first=first, chunks=chunks),
         in_specs=in_specs,
         out_specs=pl.BlockSpec(memory_space=pltpu.VMEM),
         out_shape=pltpu.VMEM(shape, jnp.bfloat16),
         input_output_aliases=aliases,
+        scratch_shapes=[
+            pltpu.VMEM((chunks, 2, fi, g, COLS), jnp.bfloat16),
+            pltpu.VMEM((chunks, 2, fr, g, COLS), jnp.bfloat16),
+            pltpu.SemaphoreType.DMA((chunks, 4)),
+        ],
         cost_estimate=pl.CostEstimate(
-            flops=flops, bytes_accessed=2 * (fi + fr) * g * 2 * COLS * steps, transcendentals=0
+            flops=flops, bytes_accessed=4 * (fi + fr) * g * COLS * chunks, transcendentals=0
         ),
-        compiler_params=pltpu.CompilerParams(vmem_limit_bytes=32 * 2**20),
+        compiler_params=pltpu.CompilerParams(vmem_limit_bytes=34 * 2**20),
     )(*args)
 
 
 def right_kernel(at_ref, z_ref, *refs, slots, final, seeded):
     refs = list(refs)
     out_ref = refs.pop()
-    total = refs.pop(0)[...] if seeded else None
+    rows = z_ref.shape[1] // 2
+    halves = [slice(0, rows), slice(rows, 2 * rows)]
+    seed = refs.pop(0) if seeded else None
+    totals = [seed[h] if seeded else None for h in halves]
     c, z, y = at_ref[0], at_ref[2], at_ref[3]
     for m_ref, (swapped, far) in zip(refs, slots):
         cls = 1 - c if swapped else c
@@ -172,16 +201,17 @@
             dz = jnp.where(cls == 0, far, near)
             dy = jnp.where(cls == 0, near, far)
             block = cls * 16 + lax.rem(z - dz + 4, 4) * 4 + lax.rem(y - dy + 4, 4)
-            part = jnp.dot(z_ref[block], m_ref[j], preferred_element_type=jnp.float32)
-            total = part if total is None else total + part
+            for i, h in enumerate(halves):
+                part = jnp.dot(z_ref[block, h], m_ref[j], preferred_element_type=jnp.float32)
+                totals[i] = part if totals[i] is None else totals[i] + part
     if final:
-        rows = total.shape[0] // 2
-        both = total[:rows] + total[rows:]
+        both = totals[0] + totals[1]
         nb = rows // 2
         out_ref[:, :nb] = both[:nb, :nb] - both[nb:, nb:]
         out_ref[:, nb:] = both[:nb, nb:] + both[nb:, :nb]
     else:
-        out_ref[...] = total
+        for i, h in enumerate(halves):
+            out_ref[h] = totals[i]
 
 
 def stack_kernel(at_ref, own_ref, first_ref, *refs):
@@ -238,17 +268,17 @@
     at = jnp.stack([c, xl, z, y, fid]).astype(jnp.int32)
     n_freq = w_imag.shape[0] + w_real.shape[0]
 
-    w_real = pltpu.with_memory_space_constraint(w_real, pltpu.HBM)
-    w_imag = pltpu.with_memory_space_constraint(w_imag, pltpu.HBM)
+    in_hbm = lambda x: pltpu.with_memory_space_constraint(x, pltpu.HBM)
+    w_imag, w_real = in_hbm(w_imag), in_hbm(w_real)
     near = []
     for k in NEAR:
         near.append(to_class_core(pair_elements, k))
     l, q = prepare(
         at,
-        pair_elements,
-        owner_bands,
-        residue_freq,
-        quad_weight,
+        in_hbm(pair_elements),
+        in_hbm(owner_bands.reshape(1, -1)),
+        in_hbm(residue_freq.reshape(1, -1)),
+        in_hbm(quad_weight),
         n_freq,
     )
     zl = left(l, q, w_imag, w_real, None, 0, FIRST)
@@ -263,8 +293,8 @@
         theirs.append(other_core(p))
 
     slots = [(s, f) for s in (False, True) for f in FAR]
-    first = right(at, zl, mine[:3] + theirs[:3], slots[:3] + slots[4:7], None, False)
-    total = right(at, zl, [mine[3], theirs[3]], [slots[3], slots[7]], first, True)
+    first = right(at, zl, mine + theirs[:1], slots[:5], None, False)
+    total = right(at, zl, theirs[1:], slots[5:], first, True)
 
     n_dev = 128
     parts = total.reshape(n_dev, 1, 2 * bands)

time: 73.3 us -> 66.4 us (0.906)
  blocking collectives: 20.9 us -> 17 us
  waiting for transfers between devices: 5.96 us -> 9.07 us
  local copies, waits for them, and re-layouts: 4.02 us -> 1.12 us
  Pallas kernels: 19.7 us -> 17.4 us
  starting transfers between devices: 21.1 us -> 20.2 us
    all_to_all x1, blocking collectives: 20.9 us -> 17 us  [on_device(): lax.all_to_all(parts, ALL, split_axis=0, concat_axis=0, tiled=True)]
    ppermute x11, waiting for transfers between devices: 5.96 us -> 9.07 us  [moved(): return lax.ppermute(x, PLANE, pairs)]
    unnamed x10 -> x2, local copies, waits for them, and re-layouts: 3.8 us -> 0.9 us
    pallas_call x2, Pallas kernels: 14.7 us -> 12.1 us  [left(): pl.pallas_call(functools.partial(left_kernel, first=first, chunks=chunks)...]
    ppermute x11, starting transfers between devices: 21.1 us -> 20.2 us  [moved(): return lax.ppermute(x, PLANE, pairs)]
  transfers between devices with their start and end apart: 11 -> 11, of which waited for: 4 -> 5; matrix products, arithmetic and copies ran while one was open for 0% -> 0% of each run, Pallas kernels for 25% -> 23%
where the time goes in v2:
time: 66.4 us; the launch traced here: 65.6 us
  starting transfers between devices  20.2 us (30%)
  Pallas kernels  17.4 us (26%)
  blocking collectives  17 us (26%)
  waiting for transfers between devices  9.07 us (14%)
  local copies, waits for them, and re-layouts  1.12 us (2%)
  other arithmetic  0.71 us (1%)
    ppermute x11, starting transfers between devices, moved(): return lax.ppermute(x, PLANE, pairs)  20.2 us
    all_to_all x1, blocking collectives, on_device(): lax.all_to_all(parts, ALL, split_axis=0, concat_axis=0, tiled=True)  17 us
    pallas_call x2, Pallas kernels, left(): pl.pallas_call(functools.partial(left_kernel, first=first, chunks=chunks)...  12.1 us
    ppermute x11, waiting for transfers between devices, moved(): return lax.ppermute(x, PLANE, pairs)  9.07 us
    pallas_call x2, Pallas kernels, right(): pl.pallas_call(functools.partial(right_kernel, slots=slots, final=final,...  3.57 us
  transfers between devices with their start and end apart: 11, of which 5 were waited for; matrix products, arithmetic and copies ran while one was open for 0% of the time, Pallas kernels for 23%

profile of v2, /device:TPU:0, one launch (start us, length us, event | category | flops | bytes accessed | tf_op | source)
XLA Modules:
  0.0 65.6 jit_solution(2731034003872811722)
XLA Ops:
  0.0 0.7 %collective-permute-start = (bf16[256,256]{1,0:T(8,128)(2,1)}, bf16[256,256]{1,0:T(8,128)(2,1)S(1)}, u32[]{:S(2)}, u32[]{:S(2)}) collective-permute-start(bf16[256,256]{1,0:T(8,128)(2,1)} %own_ref.1), channel_id=1, source_target_pairs={{32,16},{33,17},{34,18},{35,19},{36,20},{37,21},{38,22},{39,23},{4... | collective-permute-start | bytes 393224 | tf_op jit(solution)/shard_map/ppermute | solution.py:33
  0.7 1.8 %collective-permute-start.1 = (bf16[256,256]{1,0:T(8,128)(2,1)}, bf16[256,256]{1,0:T(8,128)(2,1)S(1)}, u32[]{:S(2)}, u32[]{:S(2)}) collective-permute-start(bf16[256,256]{1,0:T(8,128)(2,1)} %own_ref.1), channel_id=1, source_target_pairs={{0,1},{1,2},{2,3},{3,0},{4,5},{5,6},{6,7},{7,4},{8,9},{9,10},{10,1... | collective-permute-start | bytes 393224 | tf_op jit(solution)/shard_map/ppermute | solution.py:33
  2.4 1.5 %collective-permute-start.2 = (bf16[256,256]{1,0:T(8,128)(2,1)}, bf16[256,256]{1,0:T(8,128)(2,1)S(1)}, u32[]{:S(2)}, u32[]{:S(2)}) collective-permute-start(bf16[256,256]{1,0:T(8,128)(2,1)} %own_ref.1), channel_id=1, source_target_pairs={{0,3},{1,0},{2,1},{3,2},{4,7},{5,4},{6,5},{7,6},{8,11},{9,8},{10,9... | collective-permute-start | bytes 393224 | tf_op jit(solution)/shard_map/ppermute | solution.py:33
  4.0 2.1 %collective-permute-start.3 = (bf16[256,256]{1,0:T(8,128)(2,1)}, bf16[256,256]{1,0:T(8,128)(2,1)S(1)}, u32[]{:S(2)}, u32[]{:S(2)}) collective-permute-start(bf16[256,256]{1,0:T(8,128)(2,1)} %own_ref.1), channel_id=1, source_target_pairs={{0,2},{1,3},{2,0},{3,1},{4,6},{5,7},{6,4},{7,5},{8,10},{9,11},{10,... | collective-permute-start | bytes 393224 | tf_op jit(solution)/shard_map/ppermute | solution.py:33
  6.2 1.0 %collective-permute-done.1.refs_0_ = bf16[256,256]{1,0:T(8,128)(2,1)S(1)} collective-permute-done((bf16[256,256]{1,0:T(8,128)(2,1)}, bf16[256,256]{1,0:T(8,128)(2,1)S(1)}, u32[]{:S(2)}, u32[]{:S(2)}) %collective-permute-start.1) | collective-permute-done | bytes 131104 | tf_op jit(solution)/shard_map/ppermute | solution.py:33
  7.1 0.5 collective-permute-done.2.refs_1_
  7.6 3.1 %collective-permute-done.3.refs_2_ = bf16[256,256]{1,0:T(8,128)(2,1)S(1)} collective-permute-done((bf16[256,256]{1,0:T(8,128)(2,1)}, bf16[256,256]{1,0:T(8,128)(2,1)S(1)}, u32[]{:S(2)}, u32[]{:S(2)}) %collective-permute-start.3) | collective-permute-done | bytes 131104 | tf_op jit(solution)/shard_map/ppermute | solution.py:33
  10.7 0.9 %copy-done = bf16[256,256]{1,0:T(8,128)(2,1)S(1)} copy-done((bf16[256,256]{1,0:T(8,128)(2,1)S(1)}, bf16[256,256]{1,0:T(8,128)(2,1)}, u32[]{:S(2)}) %copy-start) | copy-done | bytes 131096
  11.6 0.6 stack.25.refs_0_
  12.2 4.2 %collective-permute-start.6 = (bf16[4,256,256]{2,1,0:T(8,128)(2,1)S(1)}, bf16[4,256,256]{2,1,0:T(8,128)(2,1)S(1)}, u32[]{:S(2)}, u32[]{:S(2)}) collective-permute-start(bf16[4,256,256]{2,1,0:T(8,128)(2,1)S(1)} %stack.25.refs_0_), channel_id=1, source_target_pairs={{0,12},{1,13},{2,14},{3,15},{4,0},{5,1},{6,2},{7,3},{8,4},{9,5},{1... | collective-permute-start | bytes 1572872 | tf_op jit(solution)/shard_map/ppermute | solution.py:33
  16.4 1.3 %collective-permute-start.5 = (bf16[4,256,256]{2,1,0:T(8,128)(2,1)S(1)}, bf16[4,256,256]{2,1,0:T(8,128)(2,1)S(1)}, u32[]{:S(2)}, u32[]{:S(2)}) collective-permute-start(bf16[4,256,256]{2,1,0:T(8,128)(2,1)S(1)} %stack.25.refs_0_), channel_id=1, source_target_pairs={{0,4},{1,5},{2,6},{3,7},{4,8},{5,9},{6,10},{7,11},{8,12},{9,13},{1... | collective-permute-start | bytes 1572872 | tf_op jit(solution)/shard_map/ppermute | solution.py:33
  17.6 1.2 %prep.1 = (bf16[256,512]{1,0:T(8,128)(2,1)S(1)}, f32[3,128,128]{2,1,0:T(8,128)S(1)}) custom-call(s32[5]{0:T(128)S(1)} %stack.24.at_ref, bf16[256,256]{1,0:T(8,128)(2,1)} %own_ref.1, s32[1,128]{1,0:T(1,128)} %bitcast.10, s32[1,128]{1,0:T(1,128)} %bitcast.11, f32[2,128]{1,0:T(2,128)} %quad_ref.1), custom_call_target="tpu_custom_call" | custom-call | tf_op jit(solution)/shard_map/prep/pallas_call | solution.py:82
  18.8 2.9 %shard_map.64.rest_0_ = bf16[32,512,256]{2,1,0:T(8,128)(2,1)S(1)} custom-call(bf16[256,512]{1,0:T(8,128)(2,1)S(1)} %get-tuple-element.7.l_ref, f32[3,128,128]{2,1,0:T(8,128)S(1)} %get-tuple-element.8.q_ref, bf16[2,256,16384]{2,1,0:T(8,128)(2,1)} %wi_ref.3, bf16[1,256,16384]{2,1,0:T(8,128)(2,1)} %wr_ref.3), custom_call_target="tpu_custom_call" | custom-call | flops 805306368 | bytes 3145728 | tf_op jit(solution)/shard_map/pallas_call | solution.py:171
  21.7 3.3 %collective-permute-start.7 = (bf16[4,256,256]{2,1,0:T(8,128)(2,1)S(1)}, bf16[4,256,256]{2,1,0:T(8,128)(2,1)S(1)}, u32[]{:S(2)}, u32[]{:S(2)}) collective-permute-start(bf16[4,256,256]{2,1,0:T(8,128)(2,1)S(1)} %stack.25.refs_0_), channel_id=1, source_target_pairs={{0,32},{1,33},{2,34},{3,35},{4,36},{5,37},{6,38},{7,39},{8,40},{9,... | collective-permute-start | bytes 1572872 | tf_op jit(solution)/shard_map/ppermute | solution.py:33
  25.0 3.7 %collective-permute-done.6.refs_3_ = bf16[4,256,256]{2,1,0:T(8,128)(2,1)S(1)} collective-permute-done((bf16[4,256,256]{2,1,0:T(8,128)(2,1)S(1)}, bf16[4,256,256]{2,1,0:T(8,128)(2,1)S(1)}, u32[]{:S(2)}, u32[]{:S(2)}) %collective-permute-start.6) | collective-permute-done | bytes 524320 | tf_op jit(solution)/shard_map/ppermute | solution.py:33
  28.7 2.8 %collective-permute-start.10 = (bf16[4,256,256]{2,1,0:T(8,128)(2,1)S(1)}, bf16[4,256,256]{2,1,0:T(8,128)(2,1)S(1)}, u32[]{:S(2)}, u32[]{:S(2)}) collective-permute-start(bf16[4,256,256]{2,1,0:T(8,128)(2,1)S(1)} %collective-permute-done.6.refs_3_), channel_id=1, source_target_pairs={{0,32},{1,33},{2,34},{3,35},{4,36},{5,37},{6,38},{7,39},{8,40},{9,... | collective-permute-start | bytes 1572872 | tf_op jit(solution)/shard_map/ppermute | solution.py:33
  31.5 0.8 %collective-permute-done.5.refs_2_ = bf16[4,256,256]{2,1,0:T(8,128)(2,1)S(1)} collective-permute-done((bf16[4,256,256]{2,1,0:T(8,128)(2,1)S(1)}, bf16[4,256,256]{2,1,0:T(8,128)(2,1)S(1)}, u32[]{:S(2)}, u32[]{:S(2)}) %collective-permute-start.5) | collective-permute-done | bytes 524320 | tf_op jit(solution)/shard_map/ppermute | solution.py:33
  32.4 2.6 %collective-permute-start.9 = (bf16[4,256,256]{2,1,0:T(8,128)(2,1)S(1)}, bf16[4,256,256]{2,1,0:T(8,128)(2,1)S(1)}, u32[]{:S(2)}, u32[]{:S(2)}) collective-permute-start(bf16[4,256,256]{2,1,0:T(8,128)(2,1)S(1)} %collective-permute-done.5.refs_2_), channel_id=1, source_target_pairs={{0,32},{1,33},{2,34},{3,35},{4,36},{5,37},{6,38},{7,39},{8,40},{9,... | collective-permute-start | bytes 1572872 | tf_op jit(solution)/shard_map/ppermute | solution.py:33
  34.9 9.2 %shard_map.65.z_ref = bf16[32,512,256]{2,1,0:T(8,128)(2,1)S(1)} custom-call(bf16[256,512]{1,0:T(8,128)(2,1)S(1)} %get-tuple-element.7.l_ref, f32[3,128,128]{2,1,0:T(8,128)S(1)} %get-tuple-element.8.q_ref, bf16[2,256,16384]{2,1,0:T(8,128)(2,1)} %wi_ref.3, bf16[1,256,16384]{2,1,0:T(8,128)(2,1)} %wr_ref.3, ...), custom_call_target="tpu_custom_call", output_to_operand_aliasing={{}: (4, {})} | custom-call | flops 5637144576 | bytes 22020096 | tf_op jit(solution)/shard_map/pallas_call | solution.py:171
  44.2 2.0 %right_first.1.refs_0_ = f32[512,256]{1,0:T(8,128)S(1)} custom-call(s32[5]{0:T(128)S(1)} %stack.24.at_ref, bf16[32,512,256]{2,1,0:T(8,128)(2,1)S(1)} %shard_map.65.z_ref, bf16[4,256,256]{2,1,0:T(8,128)(2,1)S(1)} %stack.25.refs_0_, bf16[4,256,256]{2,1,0:T(8,128)(2,1)S(1)} %collective-permute-done.4.refs_1_, ...), custom_call_target="tpu_custom_call" | custom-call | flops 1342177280 | tf_op jit(solution)/shard_map/right_first/pallas_call | solution.py:250
  46.2 1.5 %right_last.1 = f32[128,256]{1,0:T(8,128)S(1)} custom-call(s32[5]{0:T(128)S(1)} %stack.24.at_ref, bf16[32,512,256]{2,1,0:T(8,128)(2,1)S(1)} %shard_map.65.z_ref, f32[512,256]{1,0:T(8,128)S(1)} %right_first.1.refs_0_, bf16[4,256,256]{2,1,0:T(8,128)(2,1)S(1)} %collective-permute-done.8.refs_1_, bf16[4,256,256]{2,1,0:T(8,128)(2,1)S(1)} %collective-permute-done.9.refs_2_, ...), custom_call_target="tpu_custom_call" | custom-call | flops 805306368 | tf_op jit(solution)/shard_map/right_last/pallas_call | solution.py:250
  47.8 0.1 copy.8
  47.9 17.0 %all_to_all.5 = f32[128,1,256]{2,1,0:T(1,128)S(1)} all-to-all(f32[128,1,256]{2,1,0:T(1,128)S(1)} %copy.8), channel_id=1, replica_groups=mesh['xh'=2,'c'=2,'xl'=2,'z'=4,'y'=4] {'xh','c','xl','z','y'}, dimensions={0} | all-to-all | bytes 262144 | tf_op jit(solution)/shard_map/all_to_all | solution.py:301
  64.9 0.7 %reduce_sum.11 = f32[256]{0:T(256)} reduce(f32[128,1,256]{2,1,0:T(1,128)S(1)} %all_to_all.5, f32[]{:T(128)} %constant.24.clone.1), dimensions={0,1}, to_apply=%region_0.0 | reduce | flops 32512 | bytes 132100 | tf_op jit(solution)/shard_map/reduce_sum | solution.py:302
  (10 shorter events, 0.1 us)
Async XLA Ops:
  0.0 6.2 %collective-permute-start = (bf16[256,256]{1,0:T(8,128)(2,1)}, bf16[256,256]{1,0:T(8,128)(2,1)S(1)}, u32[]{:S(2)}, u32[]{:S(2)}) collective-permute-start(bf16[256,256]{1,0:T(8,128)(2,1)} %own_ref.1), channel_id=1, source_target_pairs={{32,16},{33,17},{34,18},{35,19},{36,20},{37,21},{38,22},{39,23},{4... | collective-permute-start | bytes 393224 | tf_op jit(solution)/shard_map/ppermute | solution.py:33
  0.7 6.5 %collective-permute-start.1 = (bf16[256,256]{1,0:T(8,128)(2,1)}, bf16[256,256]{1,0:T(8,128)(2,1)S(1)}, u32[]{:S(2)}, u32[]{:S(2)}) collective-permute-start(bf16[256,256]{1,0:T(8,128)(2,1)} %own_ref.1), channel_id=1, source_target_pairs={{0,1},{1,2},{2,3},{3,0},{4,5},{5,6},{6,7},{7,4},{8,9},{9,10},{10,1... | collective-permute-start | bytes 393224 | tf_op jit(solution)/shard_map/ppermute | solution.py:33
  2.4 5.2 %collective-permute-start.2 = (bf16[256,256]{1,0:T(8,128)(2,1)}, bf16[256,256]{1,0:T(8,128)(2,1)S(1)}, u32[]{:S(2)}, u32[]{:S(2)}) collective-permute-start(bf16[256,256]{1,0:T(8,128)(2,1)} %own_ref.1), channel_id=1, source_target_pairs={{0,3},{1,0},{2,1},{3,2},{4,7},{5,4},{6,5},{7,6},{8,11},{9,8},{10,9... | collective-permute-start | bytes 393224 | tf_op jit(solution)/shard_map/ppermute | solution.py:33
  4.0 6.7 %collective-permute-start.3 = (bf16[256,256]{1,0:T(8,128)(2,1)}, bf16[256,256]{1,0:T(8,128)(2,1)S(1)}, u32[]{:S(2)}, u32[]{:S(2)}) collective-permute-start(bf16[256,256]{1,0:T(8,128)(2,1)} %own_ref.1), channel_id=1, source_target_pairs={{0,2},{1,3},{2,0},{3,1},{4,6},{5,7},{6,4},{7,5},{8,10},{9,11},{10,... | collective-permute-start | bytes 393224 | tf_op jit(solution)/shard_map/ppermute | solution.py:33
  10.7 0.9 %copy-start = (bf16[256,256]{1,0:T(8,128)(2,1)S(1)}, bf16[256,256]{1,0:T(8,128)(2,1)}, u32[]{:S(2)}) copy-start(bf16[256,256]{1,0:T(8,128)(2,1)} %own_ref.1) | copy-start | bytes 393220
  12.2 16.5 %collective-permute-start.6 = (bf16[4,256,256]{2,1,0:T(8,128)(2,1)S(1)}, bf16[4,256,256]{2,1,0:T(8,128)(2,1)S(1)}, u32[]{:S(2)}, u32[]{:S(2)}) collective-permute-start(bf16[4,256,256]{2,1,0:T(8,128)(2,1)S(1)} %stack.25.refs_0_), channel_id=1, source_target_pairs={{0,12},{1,13},{2,14},{3,15},{4,0},{5,1},{6,2},{7,3},{8,4},{9,5},{1... | collective-permute-start | bytes 1572872 | tf_op jit(solution)/shard_map/ppermute | solution.py:33
  16.4 15.2 %collective-permute-start.4 = (bf16[4,256,256]{2,1,0:T(8,128)(2,1)S(1)}, bf16[4,256,256]{2,1,0:T(8,128)(2,1)S(1)}, u32[]{:S(2)}, u32[]{:S(2)}) collective-permute-start(bf16[4,256,256]{2,1,0:T(8,128)(2,1)S(1)} %stack.25.refs_0_), channel_id=1, source_target_pairs={{0,8},{1,9},{2,10},{3,11},{4,12},{5,13},{6,14},{7,15},{8,0},{9,1},... | collective-permute-start | bytes 1572872 | tf_op jit(solution)/shard_map/ppermute | solution.py:33
  16.4 16.0 %collective-permute-start.5 = (bf16[4,256,256]{2,1,0:T(8,128)(2,1)S(1)}, bf16[4,256,256]{2,1,0:T(8,128)(2,1)S(1)}, u32[]{:S(2)}, u32[]{:S(2)}) collective-permute-start(bf16[4,256,256]{2,1,0:T(8,128)(2,1)S(1)} %stack.25.refs_0_), channel_id=1, source_target_pairs={{0,4},{1,5},{2,6},{3,7},{4,8},{5,9},{6,10},{7,11},{8,12},{9,13},{1... | collective-permute-start | bytes 1572872 | tf_op jit(solution)/shard_map/ppermute | solution.py:33
  21.7 22.4 %collective-permute-start.7 = (bf16[4,256,256]{2,1,0:T(8,128)(2,1)S(1)}, bf16[4,256,256]{2,1,0:T(8,128)(2,1)S(1)}, u32[]{:S(2)}, u32[]{:S(2)}) collective-permute-start(bf16[4,256,256]{2,1,0:T(8,128)(2,1)S(1)} %stack.25.refs_0_), channel_id=1, source_target_pairs={{0,32},{1,33},{2,34},{3,35},{4,36},{5,37},{6,38},{7,39},{8,40},{9,... | collective-permute-start | bytes 1572872 | tf_op jit(solution)/shard_map/ppermute | solution.py:33
  28.7 17.5 %collective-permute-start.10 = (bf16[4,256,256]{2,1,0:T(8,128)(2,1)S(1)}, bf16[4,256,256]{2,1,0:T(8,128)(2,1)S(1)}, u32[]{:S(2)}, u32[]{:S(2)}) collective-permute-start(bf16[4,256,256]{2,1,0:T(8,128)(2,1)S(1)} %collective-permute-done.6.refs_3_), channel_id=1, source_target_pairs={{0,32},{1,33},{2,34},{3,35},{4,36},{5,37},{6,38},{7,39},{8,40},{9,... | collective-permute-start | bytes 1572872 | tf_op jit(solution)/shard_map/ppermute | solution.py:33
  31.5 14.7 %collective-permute-start.8 = (bf16[4,256,256]{2,1,0:T(8,128)(2,1)S(1)}, bf16[4,256,256]{2,1,0:T(8,128)(2,1)S(1)}, u32[]{:S(2)}, u32[]{:S(2)}) collective-permute-start(bf16[4,256,256]{2,1,0:T(8,128)(2,1)S(1)} %collective-permute-done.4.refs_1_), channel_id=1, source_target_pairs={{0,32},{1,33},{2,34},{3,35},{4,36},{5,37},{6,38},{7,39},{8,40},{9,... | collective-permute-start | bytes 1572872 | tf_op jit(solution)/shard_map/ppermute | solution.py:33
  32.4 13.9 %collective-permute-start.9 = (bf16[4,256,256]{2,1,0:T(8,128)(2,1)S(1)}, bf16[4,256,256]{2,1,0:T(8,128)(2,1)S(1)}, u32[]{:S(2)}, u32[]{:S(2)}) collective-permute-start(bf16[4,256,256]{2,1,0:T(8,128)(2,1)S(1)} %collective-permute-done.5.refs_2_), channel_id=1, source_target_pairs={{0,32},{1,33},{2,34},{3,35},{4,36},{5,37},{6,38},{7,39},{8,40},{9,... | collective-permute-start | bytes 1572872 | tf_op jit(solution)/shard_map/ppermute | solution.py:33

commit v3 on v2

v3 whole, which is shorter than its diff:
```python
import functools
from typing import NamedTuple
import jax
import jax.numpy as jnp
from jax import lax
from jax.experimental import pallas as pl
from jax.experimental.pallas import tpu as pltpu
from jax.sharding import Mesh
from jax.sharding import PartitionSpec as P


NAMES = ("xh", "c", "xl", "z", "y")
PLANE = ("c", "xl", "z", "y")
ALL = NAMES
COLS = 1024
TICK = 40_000_000_000
NEAR = (0, 1, 3, 2)
FAR = (0, 2, 1, 3)


def device_id(xl, c, z, y):
    return ((c * 2 + xl) * 4 + z % 4) * 4 + y % 4


def moved(x, target):
    pairs = []
    for xl in range(2):
        for c in range(2):
            for z in range(4):
                for y in range(4):
                    to = target(xl, c, z, y)
                    if to is not None:
                        pairs.append((device_id(xl, c, z, y), device_id(*to)))
    return lax.ppermute(x, PLANE, pairs)


def to_class_core(x, k):
    def target(xl, c, z, y):
        if c == xl and k == 0:
            return None
        at = xl if c == xl else 1 - xl
        return (at, xl, z, y + k) if xl == 0 else (at, xl, z + k, y)

    return moved(x, target)


def along_other(x, k):
    return moved(x, lambda xl, c, z, y: (xl, c, z + k, y) if c == 0 else (xl, c, z, y + k))


def other_core(x):
    return moved(x, lambda xl, c, z, y: (xl, 1 - c, z, y))


def prep_kernel(tick_ref, m_ref, owner_ref, residue_ref, quad_ref, l_ref, q_ref, copy_ref):
    nb = owner_ref.shape[1]
    owner = jnp.broadcast_to(owner_ref[...].astype(jnp.float32), (nb, nb)).T
    lanes = lax.broadcasted_iota(jnp.int32, (nb, nb), 1)
    copy_ref[...] = m_ref[...]
    pick = (owner.astype(jnp.int32) == lanes).astype(jnp.float32)
    pick16 = pick.astype(jnp.bfloat16)
    nt = (((1,), (1,)), ((), ()))
    g = m_ref.shape[0]
    re = lax.dot_general(pick16, m_ref[:, :nb], nt, preferred_element_type=jnp.float32)
    im = lax.dot_general(pick16, m_ref[:, nb:], nt, preferred_element_type=jnp.float32)
    l_ref[:nb, :g] = re.astype(jnp.bfloat16)
    l_ref[:nb, g:] = im.astype(jnp.bfloat16)
    l_ref[nb:, :g] = (-im).astype(jnp.bfloat16)
    l_ref[nb:, g:] = re.astype(jnp.bfloat16)
    nq = quad_ref.shape[0]
    fid = lax.axis_index(("xh", "c")) * (q_ref.shape[0] - nq)
    rows = [quad_ref[f : f + 1, :] for f in range(nq)]
    for r in range(q_ref.shape[0] - nq):
        rows.append((residue_ref[...] == fid + r).astype(jnp.float32))
    for f, row in enumerate(rows):
        weight = jnp.sum(pick * row, axis=1, keepdims=True)
        q_ref[f] = jnp.broadcast_to(weight, (nb, nb))


def prepare(ticked, m, owner, residue, quad, n_freq):
    g, width = m.shape
    nb = width // 2
    whole = lambda *shape: pl.BlockSpec(shape, lambda i: (0,) * len(shape))
    return pl.pallas_call(
        prep_kernel,
        grid=(1,),
        in_specs=[
            pl.BlockSpec(memory_space=pltpu.VMEM),
            whole(g, width),
            whole(1, nb),
            whole(1, nb),
            whole(*quad.shape),
        ],
        out_specs=[whole(2 * nb, 2 * g), whole(n_freq, nb, nb), whole(g, width)],
        out_shape=[
            jax.ShapeDtypeStruct((2 * nb, 2 * g), jnp.bfloat16),
            jax.ShapeDtypeStruct((n_freq, nb, nb), jnp.float32),
            jax.ShapeDtypeStruct(m.shape, m.dtype),
        ],
        compiler_params=pltpu.CompilerParams(vmem_limit_bytes=8 * 2**20),
        name="prep",
    )(ticked, m, owner, residue, quad)


def left_kernel(*refs, job):
    refs = list(refs)
    l_ref, q_ref, wi_ref, wr_ref = refs[:4]
    sem, buf = refs.pop(), refs.pop() if job.fetched else None
    ahead_ref = refs.pop() if job.ahead else None
    z_ref = refs.pop()
    ready_ref = refs[4] if job.ready else None
    g, width = wi_ref.shape[1:]
    half = width // 2
    nb = q_ref.shape[1]
    blk = z_ref.shape[2]
    c = lax.axis_index("c")

    def base(own):
        return (c if own else 1 - c) * (half // 2)

    def copies(own, chunk, dst, at):
        col = base(own) + chunk * COLS
        return [
            pltpu.make_async_copy(
                wi_ref.at[:, :, pl.ds(pl.multiple_of(part * half + col, COLS), COLS)],
                dst.at[part],
                sem.at[at, part],
            )
            for part in range(2)
        ]

    now = [copies(job.own, job.first + job.ready + j, buf.at[j], j) for j in range(job.fetched)]
    later = [
        copies(job.ahead_own, job.ahead_first + j, ahead_ref.at[j], job.fetched + j)
        for j in range(job.ahead)
    ]
    for pair in now + later:
        for copy in pair:
            copy.start()

    for j in range(job.ready + job.fetched):
        if j < job.ready:
            src = ready_ref.at[j]
        else:
            src = buf.at[j - job.ready]
            for copy in now[j - job.ready]:
                copy.wait()
        for s in range(COLS // blk):
            cols = pl.ds(s * blk, blk)
            col = base(job.own) + (job.first + j) * COLS + s * blk
            pieces = [(src[0, k, :, cols], src[1, k, :, cols]) for k in range(wi_ref.shape[0])]
            pieces += [
                (
                    wr_ref[k, :, pl.ds(pl.multiple_of(col, blk), blk)],
                    wr_ref[k, :, pl.ds(pl.multiple_of(half + col, blk), blk)],
                )
                for k in range(wr_ref.shape[0])
            ]
            total = None
            for f, (re, im) in enumerate(pieces):
                part = jnp.dot(l_ref[:, :g], re, preferred_element_type=jnp.float32)
                part = part + jnp.dot(l_ref[:, g:], im, preferred_element_type=jnp.float32)
                weight = jnp.concatenate([q_ref[f]] * (blk // nb), axis=1)
                weight = jnp.concatenate([weight, weight], axis=0)
                total = part * weight if total is None else total + part * weight
            z_ref[j * (COLS // blk) + s] = total
    for pair in later:
        for copy in pair:
            copy.wait()


class Job(NamedTuple):
    own: bool
    first: int
    ready: int
    fetched: int
    ahead_own: bool = False
    ahead_first: int = 0
    ahead: int = 0


def left(l, q, w_imag, w_real, ready, job):
    fi, g, _ = w_imag.shape
    nb = q.shape[1]
    blk = 2 * nb
    chunks = job.ready + job.fetched
    in_specs = [
        pl.BlockSpec(memory_space=pltpu.VMEM),
        pl.BlockSpec(memory_space=pltpu.VMEM),
        pl.BlockSpec(memory_space=pltpu.HBM),
        pl.BlockSpec(memory_space=pltpu.VMEM),
    ]
    args = [l, q, w_imag, w_real]
    if job.ready:
        in_specs.append(pl.BlockSpec(memory_space=pltpu.VMEM))
        args.append(ready)
    out_shape = [pltpu.VMEM((chunks * COLS // blk, 2 * nb, blk), jnp.float32)]
    if job.ahead:
        out_shape.append(pltpu.VMEM((job.ahead, 2, fi, g, COLS), jnp.bfloat16))
    scratch = [pltpu.SemaphoreType.DMA((job.fetched + job.ahead, 2))]
    if job.fetched:
        scratch.insert(0, pltpu.VMEM((job.fetched, 2, fi, g, COLS), jnp.bfloat16))
    flops = 2 * (fi + w_real.shape[0]) * 2 * nb * 2 * g * COLS * chunks
    return pl.pallas_call(
        functools.partial(left_kernel, job=job),
        in_specs=in_specs,
        out_specs=[pl.BlockSpec(memory_space=pltpu.VMEM) for _ in out_shape],
        out_shape=out_shape,
        scratch_shapes=scratch,
        cost_estimate=pl.CostEstimate(flops=flops, bytes_accessed=0, transcendentals=0),
        compiler_params=pltpu.CompilerParams(vmem_limit_bytes=8 * 2**20),
    )(*args)


def tick_kernel(out_ref):
    out_ref[...] = jnp.zeros_like(out_ref)


def tick():
    return pl.pallas_call(
        tick_kernel,
        out_specs=pl.BlockSpec(memory_space=pltpu.VMEM),
        out_shape=jax.ShapeDtypeStruct((8, 128), jnp.float32),
        cost_estimate=pl.CostEstimate(flops=TICK, bytes_accessed=0, transcendentals=0),
        compiler_params=pltpu.CompilerParams(vmem_limit_bytes=2**20),
        name="tick",
    )()


def products(z_ref, m_refs, fars):
    c, z, y = (lax.axis_index(a) for a in ("c", "z", "y"))
    totals = [None, None]
    for m_ref, far in zip(m_refs, fars):
        blocks = []
        for near in NEAR:
            dz = jnp.where(c == 0, far, near)
            dy = jnp.where(c == 0, near, far)
            blocks.append(lax.rem(z - dz + 4, 4) * 4 + lax.rem(y - dy + 4, 4))
        right_side = jnp.concatenate([m_ref[j] for j in range(m_ref.shape[0])], axis=0)
        for i in range(2):
            left_side = jnp.concatenate([z_ref[i, b] for b in blocks], axis=1)
            part = jnp.dot(left_side, right_side, preferred_element_type=jnp.float32)
            totals[i] = part if totals[i] is None else totals[i] + part
    return totals[0] + totals[1]


def join_kernel(mine_ref, early_ref, late_ref, m_ref, z_ref, sum_ref):
    early = early_ref.shape[0]
    for k in range(mine_ref.shape[0]):
        total = mine_ref[k] + (early_ref[k] if k < early else late_ref[k - early])
        hi = total.astype(jnp.bfloat16)
        z_ref[0, k] = hi
        z_ref[1, k] = (total - hi.astype(jnp.float32)).astype(jnp.bfloat16)
    sum_ref[...] = products(z_ref, [m_ref], FAR[:1])


def right_kernel(z_ref, sum_ref, *refs):
    out_ref = refs[-1]
    nb = out_ref.shape[0]
    both = sum_ref[...] + products(z_ref, refs[:-1], FAR[1:])
    out_ref[:, :nb] = both[:nb, :nb] - both[nb:, nb:]
    out_ref[:, nb:] = both[:nb, nb:] + both[nb:, :nb]


def stack_kernel(source_ref, own_ref, first_ref, *refs):
    del source_ref
    out_ref = refs[-1]
    mine = lax.axis_index("c") == lax.axis_index("xl")

    @pl.when(mine)
    def _():
        out_ref[0] = own_ref[...]

    @pl.when(jnp.logical_not(mine))
    def _():
        out_ref[0] = first_ref[...]

    for k, ref in enumerate(refs[:-1]):
        out_ref[k + 1] = ref[...]


def stack(source, own, near):
    return pl.pallas_call(
        stack_kernel,
        in_specs=[pl.BlockSpec(memory_space=pltpu.HBM)]
        + [pl.BlockSpec(memory_space=pltpu.VMEM) for _ in range(1 + len(near))],
        out_specs=pl.BlockSpec(memory_space=pltpu.VMEM),
        out_shape=jax.ShapeDtypeStruct((len(near),) + own.shape, own.dtype),
        compiler_params=pltpu.CompilerParams(vmem_limit_bytes=4 * 2**20),
        name="stack",
    )(source, own, *near)


def join(mine, early, late, four):
    n, rows, cols = mine.shape
    args = [mine, early, late, four]
    return pl.pallas_call(
        join_kernel,
        in_specs=[pl.BlockSpec(memory_space=pltpu.VMEM) for _ in args],
        out_specs=[pl.BlockSpec(memory_space=pltpu.VMEM) for _ in range(2)],
        out_shape=[
            pltpu.VMEM((2, n, rows, cols), jnp.bfloat16),
            jax.ShapeDtypeStruct((rows, cols), jnp.float32),
        ],
        cost_estimate=pl.CostEstimate(flops=2 * 10**9, bytes_accessed=0, transcendentals=0),
        compiler_params=pltpu.CompilerParams(vmem_limit_bytes=4 * 2**20),
        name="join",
    )(*args)


def right(z, part, pieces):
    rows, cols = part.shape
    args = [z, part] + list(pieces)
    return pl.pallas_call(
        right_kernel,
        in_specs=[pl.BlockSpec(memory_space=pltpu.VMEM) for _ in args],
        out_specs=pl.BlockSpec(memory_space=pltpu.VMEM),
        out_shape=jax.ShapeDtypeStruct((rows // 2, cols), jnp.float32),
        cost_estimate=pl.CostEstimate(flops=2 * 10**9, bytes_accessed=0, transcendentals=0),
        compiler_params=pltpu.CompilerParams(vmem_limit_bytes=4 * 2**20),
        name="right",
    )(*args)


def on_device(w_imag, w_real, pair_elements, quad_weight, residue_freq, owner_bands):
    bands = pair_elements.shape[1] // 2
    n_freq = w_imag.shape[0] + w_real.shape[0]

    in_hbm = lambda x: pltpu.with_memory_space_constraint(x, pltpu.HBM)
    w_imag = in_hbm(w_imag)
    w_real = pltpu.with_memory_space_constraint(w_real, pltpu.VMEM)
    ticked = tick()
    near = []
    for k in NEAR:
        near.append(to_class_core(pair_elements, k))
    l, q, m_here = prepare(
        ticked,
        in_hbm(pair_elements),
        in_hbm(owner_bands.reshape(1, -1)),
        in_hbm(residue_freq.reshape(1, -1)),
        in_hbm(quad_weight),
        n_freq,
    )
    w = (l, q, w_imag, w_real)
    early, ahead = left(*w, None, Job(False, 0, 0, 2, False, 2, 2))
    four = stack(pair_elements, m_here, near)
    far = {}
    for k in FAR[1:]:
        far[k] = along_other(four, k)
    early = other_core(early)
    late, ahead = left(*w, ahead, Job(False, 2, 2, 0, True, 0, 2))
    late = other_core(late)
    (mine,) = left(*w, ahead, Job(True, 0, 2, 2))
    z, part = join(mine, early, late, four)
    total = right(z, part, [far[k] for k in FAR[1:]])

    n_dev = 128
    parts = total.reshape(n_dev, 1, 2 * bands)
    arrived = lax.all_to_all(parts, ALL, split_axis=0, concat_axis=0, tiled=True)
    return arrived.sum(axis=0)


def solution(mesh):
    torus = Mesh(mesh.devices.reshape(2, 2, 2, 4, 4), NAMES)
    freq, gblk = ("xh", "c"), ("xl", "z", "y")
    placed = (
        P(freq, gblk, None),
        P(freq, gblk, None),
        P(gblk, None),
        P(freq, None),
        P(),
        P(),
    )
    return jax.shard_map(
        on_device, mesh=torus, in_specs=placed, out_specs=P(NAMES, None), check_vma=False
    )
```

time: 66.4 us -> 64.6 us (0.973)
  starting transfers between devices: 20.2 us -> 13.9 us
  blocking collectives: 17 us -> 21.9 us
  local copies, waits for them, and re-layouts: 1.12 us -> 2.3 us
  waiting for transfers between devices: 9.07 us -> 8.03 us
    ppermute x11 -> x9, starting transfers between devices: 20.2 us -> 13.9 us  [moved(): return lax.ppermute(x, PLANE, pairs)]
    all_to_all x1, blocking collectives: 17 us -> 21.9 us  [on_device(): lax.all_to_all(parts, ALL, split_axis=0, concat_axis=0, tiled=True)]
    unnamed x2 -> x4, local copies, waits for them, and re-layouts: 0.9 us -> 2.17 us
    ppermute x11 -> x9, waiting for transfers between devices: 9.07 us -> 8.03 us  [moved(): return lax.ppermute(x, PLANE, pairs)]
    pallas_call x5 -> x7, Pallas kernels: 16.2 us -> 15.5 us  [the longest x3 13 us: left(): pl.pallas_call(functools.partial(left_kernel, job=job), in_specs=in_specs...]
  transfers between devices with their start and end apart: 11 -> 9, of which waited for: 5 -> 5; matrix products, arithmetic and copies ran while one was open for 0% -> 0% of each run, Pallas kernels for 23% -> 11%
where the time goes in v3:
time: 64.6 us; the launch traced here: 63.8 us
  blocking collectives  21.9 us (34%)
  Pallas kernels  16.9 us (26%)
  starting transfers between devices  13.9 us (22%)
  waiting for transfers between devices  8.03 us (12%)
  local copies, waits for them, and re-layouts  2.3 us (4%)
  other arithmetic  0.71 us (1%)
    all_to_all x1, blocking collectives, on_device(): lax.all_to_all(parts, ALL, split_axis=0, concat_axis=0, tiled=True)  21.9 us
    ppermute x9, starting transfers between devices, moved(): return lax.ppermute(x, PLANE, pairs)  13.9 us
    pallas_call x3, Pallas kernels, left(): pl.pallas_call(functools.partial(left_kernel, job=job), in_specs=in_specs...  13 us
    ppermute x9, waiting for transfers between devices, moved(): return lax.ppermute(x, PLANE, pairs)  8.03 us
    unnamed x4, local copies, waits for them, and re-layouts  2.17 us
    pallas_call x1, Pallas kernels, join(): pl.pallas_call(join_kernel, in_specs=[pl.BlockSpec(memory_space=pltpu.VME...  1.49 us
    pallas_call x1, Pallas kernels, prepare(): pl.pallas_call(prep_kernel, grid=(1,), in_specs=[pl.BlockSpec(memory_spac...  1.32 us
  transfers between devices with their start and end apart: 9, of which 5 were waited for; matrix products, arithmetic and copies ran while one was open for 0% of the time, Pallas kernels for 11%

profile of v3, /device:TPU:0, one launch (start us, length us, event | category | flops | bytes accessed | tf_op | source)
XLA Modules:
  0.0 63.8 jit_solution(9358533530101515770)
XLA Ops:
  0.0 1.3 %prep.1 = (bf16[256,512]{1,0:T(8,128)(2,1)S(1)}, f32[3,128,128]{2,1,0:T(8,128)S(1)}, bf16[256,256]{1,0:T(8,128)(2,1)S(1)}) custom-call(f32[8,128]{1,0:T(8,128)S(1)} %tick.1.tick_ref, bf16[256,256]{1,0:T(8,128)(2,1)} %source_ref.1, s32[1,128]{1,0:T(1,128)} %bitcast.5, s32[1,128]{1,0:T(1,128)} %bitcast.6, f32[2,128]{1,0:T(2,128)} %quad_ref.1), custom_call_target="tpu_custom_call" | custom-call | tf_op jit(solution)/shard_map/prep/pallas_call | solution.py:84
  1.3 2.2 %copy-done = bf16[1,256,16384]{2,1,0:T(8,128)(2,1)S(1)} copy-done((bf16[1,256,16384]{2,1,0:T(8,128)(2,1)S(1)}, bf16[1,256,16384]{2,1,0:T(8,128)(2,1)}, u32[]{:S(2)}) %copy-start) | copy-done | bytes 8388632
  3.5 3.7 %shard_map.64 = (f32[8,256,256]{2,1,0:T(8,128)S(1)}, bf16[2,2,2,256,1024]{4,3,2,1,0:T(8,128)(2,1)S(1)}) custom-call(bf16[256,512]{1,0:T(8,128)(2,1)S(1)} %get-tuple-element.14.refs_0_, f32[3,128,128]{2,1,0:T(8,128)S(1)} %get-tuple-element.15.refs_1_, bf16[2,256,16384]{2,1,0:T(8,128)(2,1)} %refs_2_.5, bf16[1,256,16384]{2,1,0:T(8,128)(2,1)S(1)} %copy-done), custom_call_target="tpu_custom_call" | custom-call | flops 1610612736 | tf_op jit(solution)/shard_map/pallas_call | solution.py:204
  7.2 3.9 %shard_map.65 = (f32[8,256,256]{2,1,0:T(8,128)S(1)}, bf16[2,2,2,256,1024]{4,3,2,1,0:T(8,128)(2,1)S(1)}) custom-call(bf16[256,512]{1,0:T(8,128)(2,1)S(1)} %get-tuple-element.14.refs_0_, f32[3,128,128]{2,1,0:T(8,128)S(1)} %get-tuple-element.15.refs_1_, bf16[2,256,16384]{2,1,0:T(8,128)(2,1)} %refs_2_.5, bf16[1,256,16384]{2,1,0:T(8,128)(2,1)S(1)} %copy-done, ...), custom_call_target="tpu_custom_call" | custom-call | flops 1610612736 | tf_op jit(solution)/shard_map/pallas_call | solution.py:204
  11.1 0.1 collective-permute-start.1
  11.2 0.5 collective-permute-start
  11.7 0.7 %collective-permute-start.2 = (bf16[256,256]{1,0:T(8,128)(2,1)S(1)}, bf16[256,256]{1,0:T(8,128)(2,1)S(1)}, u32[]{:S(2)}, u32[]{:S(2)}) collective-permute-start(bf16[256,256]{1,0:T(8,128)(2,1)S(1)} %copy-done.1), channel_id=1, source_target_pairs={{32,16},{33,17},{34,18},{35,19},{36,20},{37,21},{38,22},{39,23},{4... | collective-permute-start | bytes 393224 | tf_op jit(solution)/shard_map/ppermute | solution.py:34
  12.4 1.8 %collective-permute-start.3 = (bf16[256,256]{1,0:T(8,128)(2,1)S(1)}, bf16[256,256]{1,0:T(8,128)(2,1)S(1)}, u32[]{:S(2)}, u32[]{:S(2)}) collective-permute-start(bf16[256,256]{1,0:T(8,128)(2,1)S(1)} %copy-done.1), channel_id=1, source_target_pairs={{0,1},{1,2},{2,3},{3,0},{4,5},{5,6},{6,7},{7,4},{8,9},{9,10},{10,1... | collective-permute-start | bytes 393224 | tf_op jit(solution)/shard_map/ppermute | solution.py:34
  14.2 1.5 %collective-permute-start.4 = (bf16[256,256]{1,0:T(8,128)(2,1)S(1)}, bf16[256,256]{1,0:T(8,128)(2,1)S(1)}, u32[]{:S(2)}, u32[]{:S(2)}) collective-permute-start(bf16[256,256]{1,0:T(8,128)(2,1)S(1)} %copy-done.1), channel_id=1, source_target_pairs={{0,3},{1,0},{2,1},{3,2},{4,7},{5,4},{6,5},{7,6},{8,11},{9,8},{10,9... | collective-permute-start | bytes 393224 | tf_op jit(solution)/shard_map/ppermute | solution.py:34
  15.7 2.1 %collective-permute-start.5 = (bf16[256,256]{1,0:T(8,128)(2,1)S(1)}, bf16[256,256]{1,0:T(8,128)(2,1)S(1)}, u32[]{:S(2)}, u32[]{:S(2)}) collective-permute-start(bf16[256,256]{1,0:T(8,128)(2,1)S(1)} %copy-done.1), channel_id=1, source_target_pairs={{0,2},{1,3},{2,0},{3,1},{4,6},{5,7},{6,4},{7,5},{8,10},{9,11},{10,... | collective-permute-start | bytes 393224 | tf_op jit(solution)/shard_map/ppermute | solution.py:34
  17.8 0.8 %collective-permute-done.3.refs_0_ = bf16[256,256]{1,0:T(8,128)(2,1)S(1)} collective-permute-done((bf16[256,256]{1,0:T(8,128)(2,1)S(1)}, bf16[256,256]{1,0:T(8,128)(2,1)S(1)}, u32[]{:S(2)}, u32[]{:S(2)}) %collective-permute-start.3) | collective-permute-done | bytes 131104 | tf_op jit(solution)/shard_map/ppermute | solution.py:34
  18.7 0.5 collective-permute-done.4.refs_1_
  19.1 3.0 %collective-permute-done.5.refs_2_ = bf16[256,256]{1,0:T(8,128)(2,1)S(1)} collective-permute-done((bf16[256,256]{1,0:T(8,128)(2,1)S(1)}, bf16[256,256]{1,0:T(8,128)(2,1)S(1)}, u32[]{:S(2)}, u32[]{:S(2)}) %collective-permute-start.5) | collective-permute-done | bytes 131104 | tf_op jit(solution)/shard_map/ppermute | solution.py:34
  22.2 4.1 %collective-permute-start.6 = (bf16[4,256,256]{2,1,0:T(8,128)(2,1)S(1)}, bf16[4,256,256]{2,1,0:T(8,128)(2,1)S(1)}, u32[]{:S(2)}, u32[]{:S(2)}) collective-permute-start(bf16[4,256,256]{2,1,0:T(8,128)(2,1)S(1)} %stack.1.m_ref), channel_id=1, source_target_pairs={{0,8},{1,9},{2,10},{3,11},{4,12},{5,13},{6,14},{7,15},{8,0},{9,1},... | collective-permute-start | bytes 1572872 | tf_op jit(solution)/shard_map/ppermute | solution.py:34
  26.3 1.0 %collective-permute-start.7 = (bf16[4,256,256]{2,1,0:T(8,128)(2,1)S(1)}, bf16[4,256,256]{2,1,0:T(8,128)(2,1)S(1)}, u32[]{:S(2)}, u32[]{:S(2)}) collective-permute-start(bf16[4,256,256]{2,1,0:T(8,128)(2,1)S(1)} %stack.1.m_ref), channel_id=1, source_target_pairs={{0,4},{1,5},{2,6},{3,7},{4,8},{5,9},{6,10},{7,11},{8,12},{9,13},{1... | collective-permute-start | bytes 1572872 | tf_op jit(solution)/shard_map/ppermute | solution.py:34
  27.3 2.2 %collective-permute-start.8 = (bf16[4,256,256]{2,1,0:T(8,128)(2,1)S(1)}, bf16[4,256,256]{2,1,0:T(8,128)(2,1)S(1)}, u32[]{:S(2)}, u32[]{:S(2)}) collective-permute-start(bf16[4,256,256]{2,1,0:T(8,128)(2,1)S(1)} %stack.1.m_ref), channel_id=1, source_target_pairs={{0,12},{1,13},{2,14},{3,15},{4,0},{5,1},{6,2},{7,3},{8,4},{9,5},{1... | collective-permute-start | bytes 1572872 | tf_op jit(solution)/shard_map/ppermute | solution.py:34
  29.5 5.4 %shard_map.66.mine_ref = f32[16,256,256]{2,1,0:T(8,128)S(1)} custom-call(bf16[256,512]{1,0:T(8,128)(2,1)S(1)} %get-tuple-element.14.refs_0_, f32[3,128,128]{2,1,0:T(8,128)S(1)} %get-tuple-element.15.refs_1_, bf16[2,256,16384]{2,1,0:T(8,128)(2,1)} %refs_2_.5, bf16[1,256,16384]{2,1,0:T(8,128)(2,1)S(1)} %copy-done, ...), custom_call_target="tpu_custom_call" | custom-call | flops 3221225472 | tf_op jit(solution)/shard_map/pallas_call | solution.py:204
  35.0 1.5 %join.1 = (bf16[2,16,256,256]{3,2,1,0:T(8,128)(2,1)S(1)}, f32[256,256]{1,0:T(8,128)S(1)}) custom-call(f32[16,256,256]{2,1,0:T(8,128)S(1)} %shard_map.66.mine_ref, f32[8,256,256]{2,1,0:T(8,128)S(1)} %collective-permute-done.early_ref, f32[8,256,256]{2,1,0:T(8,128)S(1)} %collective-permute-done.1.late_ref, bf16[4,256,256]{2,1,0:T(8,128)(2,1)S(1)} %stack.1.m_ref), custom_call_target="tpu_custom_call" | custom-call | flops 2000000000 | tf_op jit(solution)/shard_map/join/pallas_call | solution.py:297
  36.5 2.7 %collective-permute-done.7.refs_1_ = bf16[4,256,256]{2,1,0:T(8,128)(2,1)S(1)} collective-permute-done((bf16[4,256,256]{2,1,0:T(8,128)(2,1)S(1)}, bf16[4,256,256]{2,1,0:T(8,128)(2,1)S(1)}, u32[]{:S(2)}, u32[]{:S(2)}) %collective-permute-start.7) | collective-permute-done | bytes 524320 | tf_op jit(solution)/shard_map/ppermute | solution.py:34
  39.2 0.9 %collective-permute-done.8.refs_2_ = bf16[4,256,256]{2,1,0:T(8,128)(2,1)S(1)} collective-permute-done((bf16[4,256,256]{2,1,0:T(8,128)(2,1)S(1)}, bf16[4,256,256]{2,1,0:T(8,128)(2,1)S(1)}, u32[]{:S(2)}, u32[]{:S(2)}) %collective-permute-start.8) | collective-permute-done | bytes 524320 | tf_op jit(solution)/shard_map/ppermute | solution.py:34
  40.1 1.0 %right.1 = f32[128,256]{1,0:T(8,128)S(1)} custom-call(bf16[2,16,256,256]{3,2,1,0:T(8,128)(2,1)S(1)} %get-tuple-element.21.z_ref, f32[256,256]{1,0:T(8,128)S(1)} %get-tuple-element.22.sum_ref, bf16[4,256,256]{2,1,0:T(8,128)(2,1)S(1)} %collective-permute-done.6.refs_0_, bf16[4,256,256]{2,1,0:T(8,128)(2,1)S(1)} %collective-permute-done.7.refs_1_, ...), custom_call_target="tpu_custom_call" | custom-call | flops 2000000000 | tf_op jit(solution)/shard_map/right/pallas_call | solution.py:314
  41.1 0.1 copy.7
  41.3 21.9 %all_to_all.5 = f32[128,1,256]{2,1,0:T(1,128)S(1)} all-to-all(f32[128,1,256]{2,1,0:T(1,128)S(1)} %copy.7), channel_id=1, replica_groups=mesh['xh'=2,'c'=2,'xl'=2,'z'=4,'y'=4] {'xh','c','xl','z','y'}, dimensions={0} | all-to-all | bytes 262144 | tf_op jit(solution)/shard_map/all_to_all | solution.py:359
  63.1 0.7 %reduce_sum.11 = f32[256]{0:T(256)} reduce(f32[128,1,256]{2,1,0:T(1,128)S(1)} %all_to_all.5, f32[]{:T(128)} %constant.0.clone.1), dimensions={0,1}, to_apply=%region_0.0 | reduce | flops 32512 | bytes 132100 | tf_op jit(solution)/shard_map/reduce_sum | solution.py:360
  (9 shorter events, 0.1 us)
Async XLA Ops:
  0.0 3.5 %copy-start = (bf16[1,256,16384]{2,1,0:T(8,128)(2,1)S(1)}, bf16[1,256,16384]{2,1,0:T(8,128)(2,1)}, u32[]{:S(2)}) copy-start(bf16[1,256,16384]{2,1,0:T(8,128)(2,1)} %refs_3_.5) | copy-start | bytes 25165828
  7.2 4.5 %copy-start.1 = (bf16[256,256]{1,0:T(8,128)(2,1)S(1)}, bf16[256,256]{1,0:T(8,128)(2,1)}, u32[]{:S(2)}) copy-start(bf16[256,256]{1,0:T(8,128)(2,1)} %source_ref.1) | copy-start | bytes 393220
  11.1 23.8 %collective-permute-start.1 = (f32[8,256,256]{2,1,0:T(8,128)S(1)}, f32[8,256,256]{2,1,0:T(8,128)S(1)}, u32[]{:S(2)}, u32[]{:S(2)}) collective-permute-start(f32[8,256,256]{2,1,0:T(8,128)S(1)} %get-tuple-element.19), channel_id=1, source_target_pairs={{0,32},{1,33},{2,34},{3,35},{4,36},{5,37},{6,38},{7,39},{8,40},{9,... | collective-permute-start | bytes 6291464 | tf_op jit(solution)/shard_map/ppermute | solution.py:34
  11.2 23.7 %collective-permute-start = (f32[8,256,256]{2,1,0:T(8,128)S(1)}, f32[8,256,256]{2,1,0:T(8,128)S(1)}, u32[]{:S(2)}, u32[]{:S(2)}) collective-permute-start(f32[8,256,256]{2,1,0:T(8,128)S(1)} %get-tuple-element.18), channel_id=1, source_target_pairs={{0,32},{1,33},{2,34},{3,35},{4,36},{5,37},{6,38},{7,39},{8,40},{9,... | collective-permute-start | bytes 6291464 | tf_op jit(solution)/shard_map/ppermute | solution.py:34
  11.7 4.0 %collective-permute-start.2 = (bf16[256,256]{1,0:T(8,128)(2,1)S(1)}, bf16[256,256]{1,0:T(8,128)(2,1)S(1)}, u32[]{:S(2)}, u32[]{:S(2)}) collective-permute-start(bf16[256,256]{1,0:T(8,128)(2,1)S(1)} %copy-done.1), channel_id=1, source_target_pairs={{32,16},{33,17},{34,18},{35,19},{36,20},{37,21},{38,22},{39,23},{4... | collective-permute-start | bytes 393224 | tf_op jit(solution)/shard_map/ppermute | solution.py:34
  12.4 6.2 %collective-permute-start.3 = (bf16[256,256]{1,0:T(8,128)(2,1)S(1)}, bf16[256,256]{1,0:T(8,128)(2,1)S(1)}, u32[]{:S(2)}, u32[]{:S(2)}) collective-permute-start(bf16[256,256]{1,0:T(8,128)(2,1)S(1)} %copy-done.1), channel_id=1, source_target_pairs={{0,1},{1,2},{2,3},{3,0},{4,5},{5,6},{6,7},{7,4},{8,9},{9,10},{10,1... | collective-permute-start | bytes 393224 | tf_op jit(solution)/shard_map/ppermute | solution.py:34
  14.2 5.0 %collective-permute-start.4 = (bf16[256,256]{1,0:T(8,128)(2,1)S(1)}, bf16[256,256]{1,0:T(8,128)(2,1)S(1)}, u32[]{:S(2)}, u32[]{:S(2)}) collective-permute-start(bf16[256,256]{1,0:T(8,128)(2,1)S(1)} %copy-done.1), channel_id=1, source_target_pairs={{0,3},{1,0},{2,1},{3,2},{4,7},{5,4},{6,5},{7,6},{8,11},{9,8},{10,9... | collective-permute-start | bytes 393224 | tf_op jit(solution)/shard_map/ppermute | solution.py:34
  15.7 6.5 %collective-permute-start.5 = (bf16[256,256]{1,0:T(8,128)(2,1)S(1)}, bf16[256,256]{1,0:T(8,128)(2,1)S(1)}, u32[]{:S(2)}, u32[]{:S(2)}) collective-permute-start(bf16[256,256]{1,0:T(8,128)(2,1)S(1)} %copy-done.1), channel_id=1, source_target_pairs={{0,2},{1,3},{2,0},{3,1},{4,6},{5,7},{6,4},{7,5},{8,10},{9,11},{10,... | collective-permute-start | bytes 393224 | tf_op jit(solution)/shard_map/ppermute | solution.py:34
  22.2 14.2 %collective-permute-start.6 = (bf16[4,256,256]{2,1,0:T(8,128)(2,1)S(1)}, bf16[4,256,256]{2,1,0:T(8,128)(2,1)S(1)}, u32[]{:S(2)}, u32[]{:S(2)}) collective-permute-start(bf16[4,256,256]{2,1,0:T(8,128)(2,1)S(1)} %stack.1.m_ref), channel_id=1, source_target_pairs={{0,8},{1,9},{2,10},{3,11},{4,12},{5,13},{6,14},{7,15},{8,0},{9,1},... | collective-permute-start | bytes 1572872 | tf_op jit(solution)/shard_map/ppermute | solution.py:34
  26.3 12.9 %collective-permute-start.7 = (bf16[4,256,256]{2,1,0:T(8,128)(2,1)S(1)}, bf16[4,256,256]{2,1,0:T(8,128)(2,1)S(1)}, u32[]{:S(2)}, u32[]{:S(2)}) collective-permute-start(bf16[4,256,256]{2,1,0:T(8,128)(2,1)S(1)} %stack.1.m_ref), channel_id=1, source_target_pairs={{0,4},{1,5},{2,6},{3,7},{4,8},{5,9},{6,10},{7,11},{8,12},{9,13},{1... | collective-permute-start | bytes 1572872 | tf_op jit(solution)/shard_map/ppermute | solution.py:34
  27.3 12.8 %collective-permute-start.8 = (bf16[4,256,256]{2,1,0:T(8,128)(2,1)S(1)}, bf16[4,256,256]{2,1,0:T(8,128)(2,1)S(1)}, u32[]{:S(2)}, u32[]{:S(2)}) collective-permute-start(bf16[4,256,256]{2,1,0:T(8,128)(2,1)S(1)} %stack.1.m_ref), channel_id=1, source_target_pairs={{0,12},{1,13},{2,14},{3,15},{4,0},{5,1},{6,2},{7,3},{8,4},{9,5},{1... | collective-permute-start | bytes 1572872 | tf_op jit(solution)/shard_map/ppermute | solution.py:34

commit v4 on v3

--- a/solution.py
+++ b/solution.py
@@ -15,7 +15,6 @@
 COLS = 1024
 TICK = 40_000_000_000
 NEAR = (0, 1, 3, 2)
-FAR = (0, 2, 1, 3)
 
 
 def device_id(xl, c, z, y):
@@ -50,6 +49,21 @@
 
 def other_core(x):
     return moved(x, lambda xl, c, z, y: (xl, 1 - c, z, y))
+
+
+def x_neighbour(x):
+    pairs = []
+    for xh in range(2):
+        for xl in range(2):
+            for c in range(2):
+                step = 1 if xl == c else -1
+                at = (2 * xh + xl + step) % 4
+                for z in range(4):
+                    for y in range(4):
+                        source = (xh * 2 + c) * 32 + (xl * 4 + z) * 4 + y
+                        target = (at // 2 * 2 + c) * 32 + (at % 2 * 4 + z) * 4 + y
+                        pairs.append((source, target))
+    return lax.ppermute(x, ALL, pairs)
 
 
 def prep_kernel(tick_ref, m_ref, owner_ref, residue_ref, quad_ref, l_ref, q_ref, copy_ref):
@@ -102,13 +116,23 @@
     )(ticked, m, owner, residue, quad)
 
 
+def split(total, z_ref, at):
+    hi = total.astype(jnp.bfloat16)
+    z_ref[0, at] = hi
+    z_ref[1, at] = (total - hi.astype(jnp.float32)).astype(jnp.bfloat16)
+
+
 def left_kernel(*refs, job):
     refs = list(refs)
-    l_ref, q_ref, wi_ref, wr_ref = refs[:4]
-    sem, buf = refs.pop(), refs.pop() if job.fetched else None
+    sem = refs.pop()
+    buf = refs.pop() if job.fetched else None
+    join_ref = refs.pop() if job.joined else None
     ahead_ref = refs.pop() if job.ahead else None
     z_ref = refs.pop()
-    ready_ref = refs[4] if job.ready else None
+    l_ref, q_ref, wi_ref, wr_ref = refs[:4]
+    refs = refs[4:]
+    ready_ref = refs.pop(0) if job.ready else None
+    early_ref = refs.pop(0) if job.joined else None
     g, width = wi_ref.shape[1:]
     half = width // 2
     nb = q_ref.shape[1]
@@ -138,13 +162,7 @@
         for copy in pair:
             copy.start()
 
-    for j in range(job.ready + job.fetched):
-        if j < job.ready:
-            src = ready_ref.at[j]
-        else:
-            src = buf.at[j - job.ready]
-            for copy in now[j - job.ready]:
-                copy.wait()
+    def chunk(j, src):
         for s in range(COLS // blk):
             cols = pl.ds(s * blk, blk)
             col = base(job.own) + (job.first + j) * COLS + s * blk
@@ -163,7 +181,24 @@
                 weight = jnp.concatenate([q_ref[f]] * (blk // nb), axis=1)
                 weight = jnp.concatenate([weight, weight], axis=0)
                 total = part * weight if total is None else total + part * weight
-            z_ref[j * (COLS // blk) + s] = total
+            at = j * (COLS // blk) + s
+            if at < job.joined:
+                split(total + early_ref[at], join_ref, at)
+            else:
+                z_ref[at - job.joined] = total
+
+    for j in range(job.ready + job.fetched):
+        if j < job.ready:
+            src = ready_ref.at[j]
+        else:
+            src = buf.at[j - job.ready]
+            for copy in now[j - job.ready]:
+                copy.wait()
+
+        @pl.when(c >= 0)
+        def _(j=j, src=src):
+            chunk(j, src)
+
     for pair in later:
         for copy in pair:
             copy.wait()
@@ -177,34 +212,34 @@
     ahead_own: bool = False
     ahead_first: int = 0
     ahead: int = 0
-
-
-def left(l, q, w_imag, w_real, ready, job):
+    joined: int = 0
+
+
+def left(lead, w_imag, w_real, extra, job):
     fi, g, _ = w_imag.shape
-    nb = q.shape[1]
+    fr = w_real.shape[0]
+    nb = g // 2
     blk = 2 * nb
     chunks = job.ready + job.fetched
-    in_specs = [
-        pl.BlockSpec(memory_space=pltpu.VMEM),
-        pl.BlockSpec(memory_space=pltpu.VMEM),
-        pl.BlockSpec(memory_space=pltpu.HBM),
-        pl.BlockSpec(memory_space=pltpu.VMEM),
-    ]
-    args = [l, q, w_imag, w_real]
-    if job.ready:
-        in_specs.append(pl.BlockSpec(memory_space=pltpu.VMEM))
-        args.append(ready)
-    out_shape = [pltpu.VMEM((chunks * COLS // blk, 2 * nb, blk), jnp.float32)]
+    blocks = chunks * COLS // blk
+    vmem = pl.BlockSpec(memory_space=pltpu.VMEM)
+    hbm = pl.BlockSpec(memory_space=pltpu.HBM)
+    in_specs = [vmem for _ in lead] + [hbm, vmem] + [vmem for _ in extra]
+    args = [*lead, w_imag, w_real, *extra]
+    out_shape = [pltpu.VMEM((blocks - job.joined, blk, blk), jnp.float32)]
+    scratch = []
     if job.ahead:
         out_shape.append(pltpu.VMEM((job.ahead, 2, fi, g, COLS), jnp.bfloat16))
-    scratch = [pltpu.SemaphoreType.DMA((job.fetched + job.ahead, 2))]
+    if job.joined:
+        out_shape.append(pltpu.VMEM((2, blocks, blk, blk), jnp.bfloat16))
     if job.fetched:
-        scratch.insert(0, pltpu.VMEM((job.fetched, 2, fi, g, COLS), jnp.bfloat16))
-    flops = 2 * (fi + w_real.shape[0]) * 2 * nb * 2 * g * COLS * chunks
+        scratch.append(pltpu.VMEM((job.fetched, 2, fi, g, COLS), jnp.bfloat16))
+    scratch.append(pltpu.SemaphoreType.DMA((job.fetched + job.ahead, 2)))
+    flops = 2 * (fi + fr) * 2 * nb * 2 * g * COLS * chunks
     return pl.pallas_call(
         functools.partial(left_kernel, job=job),
         in_specs=in_specs,
-        out_specs=[pl.BlockSpec(memory_space=pltpu.VMEM) for _ in out_shape],
+        out_specs=[vmem for _ in out_shape],
         out_shape=out_shape,
         scratch_shapes=scratch,
         cost_estimate=pl.CostEstimate(flops=flops, bytes_accessed=0, transcendentals=0),
@@ -227,12 +262,12 @@
     )()
 
 
-def products(z_ref, m_refs, fars):
+def products(z_ref, parts):
     c, z, y = (lax.axis_index(a) for a in ("c", "z", "y"))
     totals = [None, None]
-    for m_ref, far in zip(m_refs, fars):
+    for m_ref, far, nears in parts:
         blocks = []
-        for near in NEAR:
+        for near in nears:
             dz = jnp.where(c == 0, far, near)
             dy = jnp.where(c == 0, near, far)
             blocks.append(lax.rem(z - dz + 4, 4) * 4 + lax.rem(y - dy + 4, 4))
@@ -244,38 +279,47 @@
     return totals[0] + totals[1]
 
 
-def join_kernel(mine_ref, early_ref, late_ref, m_ref, z_ref, sum_ref):
-    early = early_ref.shape[0]
+def join_kernel(mine_ref, late_ref, m_ref, z_in_ref, z_ref, sum_ref):
+    del z_in_ref
+    first = z_ref.shape[1] - mine_ref.shape[0]
     for k in range(mine_ref.shape[0]):
-        total = mine_ref[k] + (early_ref[k] if k < early else late_ref[k - early])
-        hi = total.astype(jnp.bfloat16)
-        z_ref[0, k] = hi
-        z_ref[1, k] = (total - hi.astype(jnp.float32)).astype(jnp.bfloat16)
-    sum_ref[...] = products(z_ref, [m_ref], FAR[:1])
-
-
-def right_kernel(z_ref, sum_ref, *refs):
-    out_ref = refs[-1]
+        split(mine_ref[k] + late_ref[k], z_ref, first + k)
+    sum_ref[...] = products(z_ref, [(m_ref, 0, NEAR)])
+
+
+def right_kernel(z_ref, sum_ref, next_ref, last_ref, here_ref, there_ref, out_ref):
     nb = out_ref.shape[0]
-    both = sum_ref[...] + products(z_ref, refs[:-1], FAR[1:])
+    mine = lax.axis_index("c") == lax.axis_index("xl")
+    half = here_ref.shape[0]
+    lower, upper = NEAR[:half], NEAR[half:]
+    here = [jnp.where(mine, a, b) for a, b in zip(lower, upper)]
+    there = [jnp.where(mine, b, a) for a, b in zip(lower, upper)]
+    parts = [(next_ref, 1, NEAR), (last_ref, 3, NEAR), (here_ref, 2, here), (there_ref, 2, there)]
+    both = sum_ref[...] + products(z_ref, parts)
     out_ref[:, :nb] = both[:nb, :nb] - both[nb:, nb:]
     out_ref[:, nb:] = both[:nb, nb:] + both[nb:, :nb]
 
 
 def stack_kernel(source_ref, own_ref, first_ref, *refs):
     del source_ref
-    out_ref = refs[-1]
+    refs, out_ref, half_ref = refs[:-2], refs[-2], refs[-1]
     mine = lax.axis_index("c") == lax.axis_index("xl")
+    half = half_ref.shape[0]
 
     @pl.when(mine)
     def _():
         out_ref[0] = own_ref[...]
+        half_ref[0] = own_ref[...]
+        for k in range(1, half):
+            half_ref[k] = refs[k - 1][...]
 
     @pl.when(jnp.logical_not(mine))
     def _():
         out_ref[0] = first_ref[...]
-
-    for k, ref in enumerate(refs[:-1]):
+        for k in range(half):
+            half_ref[k] = refs[half + k - 1][...]
+
+    for k, ref in enumerate(refs):
         out_ref[k + 1] = ref[...]
 
 
@@ -284,24 +328,27 @@
         stack_kernel,
         in_specs=[pl.BlockSpec(memory_space=pltpu.HBM)]
         + [pl.BlockSpec(memory_space=pltpu.VMEM) for _ in range(1 + len(near))],
-        out_specs=pl.BlockSpec(memory_space=pltpu.VMEM),
-        out_shape=jax.ShapeDtypeStruct((len(near),) + own.shape, own.dtype),
+        out_specs=[pl.BlockSpec(memory_space=pltpu.VMEM) for _ in range(2)],
+        out_shape=[
+            jax.ShapeDtypeStruct((n,) + own.shape, own.dtype) for n in (len(near), len(near) // 2)
+        ],
         compiler_params=pltpu.CompilerParams(vmem_limit_bytes=4 * 2**20),
         name="stack",
     )(source, own, *near)
 
 
-def join(mine, early, late, four):
-    n, rows, cols = mine.shape
-    args = [mine, early, late, four]
+def join(mine, late, four, z):
+    rows, cols = mine.shape[1:]
+    args = [mine, late, four, z]
     return pl.pallas_call(
         join_kernel,
         in_specs=[pl.BlockSpec(memory_space=pltpu.VMEM) for _ in args],
         out_specs=[pl.BlockSpec(memory_space=pltpu.VMEM) for _ in range(2)],
         out_shape=[
-            pltpu.VMEM((2, n, rows, cols), jnp.bfloat16),
+            pltpu.VMEM(z.shape, z.dtype),
             jax.ShapeDtypeStruct((rows, cols), jnp.float32),
         ],
+        input_output_aliases={3: 0},
         cost_estimate=pl.CostEstimate(flops=2 * 10**9, bytes_accessed=0, transcendentals=0),
         compiler_params=pltpu.CompilerParams(vmem_limit_bytes=4 * 2**20),
         name="join",
@@ -324,7 +371,6 @@
 
 def on_device(w_imag, w_real, pair_elements, quad_weight, residue_freq, owner_bands):
     bands = pair_elements.shape[1] // 2
-    n_freq = w_imag.shape[0] + w_real.shape[0]
 
     in_hbm = lambda x: pltpu.with_memory_space_constraint(x, pltpu.HBM)
     w_imag = in_hbm(w_imag)
@@ -333,6 +379,7 @@
     near = []
     for k in NEAR:
         near.append(to_class_core(pair_elements, k))
+    n_freq = w_imag.shape[0] + w_real.shape[0]
     l, q, m_here = prepare(
         ticked,
         in_hbm(pair_elements),
@@ -341,18 +388,19 @@
         in_hbm(quad_weight),
         n_freq,
     )
-    w = (l, q, w_imag, w_real)
-    early, ahead = left(*w, None, Job(False, 0, 0, 2, False, 2, 2))
-    four = stack(pair_elements, m_here, near)
-    far = {}
-    for k in FAR[1:]:
-        far[k] = along_other(four, k)
+    w = ((l, q), w_imag, w_real)
+    early, ahead = left(*w, [], Job(False, 0, 0, 2, False, 2, 2))
+    four, half = stack(pair_elements, m_here, near)
+    here = along_other(half, 2)
+    next_far = along_other(four, 1)
+    last_far = along_other(four, 3)
     early = other_core(early)
-    late, ahead = left(*w, ahead, Job(False, 2, 2, 0, True, 0, 2))
+    late, ahead = left(*w, [ahead], Job(False, 2, 2, 0, True, 0, 2))
     late = other_core(late)
-    (mine,) = left(*w, ahead, Job(True, 0, 2, 2))
-    z, part = join(mine, early, late, four)
-    total = right(z, part, [far[k] for k in FAR[1:]])
+    there = x_neighbour(here)
+    mine, z = left(*w, [ahead, early], Job(True, 0, 2, 2, joined=early.shape[0]))
+    z, part = join(mine, late, four, z)
+    total = right(z, part, [next_far, last_far, here, there])
 
     n_dev = 128
     parts = total.reshape(n_dev, 1, 2 * bands)

time: 64.6 us -> 61.3 us (0.949)
  starting transfers between devices: 13.9 us -> 19.9 us
  blocking collectives: 21.9 us -> 18.3 us
  Pallas kernels: 16.9 us -> 13.5 us
  waiting for transfers between devices: 8.03 us -> 5.61 us
    ppermute x0 -> x1, starting transfers between devices: none -> 5.94 us  [x_neighbour(): return lax.ppermute(x, ALL, pairs)]
    all_to_all x1, blocking collectives: 21.9 us -> 18.3 us  [on_device(): lax.all_to_all(parts, ALL, split_axis=0, concat_axis=0, tiled=True)]
    pallas_call x3, Pallas kernels: 13 us -> 10.2 us  [left(): pl.pallas_call(functools.partial(left_kernel, job=job), in_specs=in_specs...]
    ppermute x9, waiting for transfers between devices: 8.03 us -> 5.6 us  [moved(): return lax.ppermute(x, PLANE, pairs)]
  transfers between devices with their start and end apart: 9 -> 10, of which waited for: 5 -> 4; matrix products, arithmetic and copies ran while one was open for 0% -> 0% of each run, Pallas kernels for 11% -> 12%
where the time goes in v4:
time: 61.3 us; the launch traced here: 60.5 us
  starting transfers between devices  19.9 us (32%)
  blocking collectives  18.3 us (30%)
  Pallas kernels  13.5 us (22%)
  waiting for transfers between devices  5.61 us (9%)
  local copies, waits for them, and re-layouts  2.3 us (4%)
  other arithmetic  0.71 us (1%)
    all_to_all x1, blocking collectives, on_device(): lax.all_to_all(parts, ALL, split_axis=0, concat_axis=0, tiled=True)  18.3 us
    ppermute x9, starting transfers between devices, moved(): return lax.ppermute(x, PLANE, pairs)  14 us
    pallas_call x3, Pallas kernels, left(): pl.pallas_call(functools.partial(left_kernel, job=job), in_specs=in_specs...  10.2 us
    ppermute x1, starting transfers between devices, x_neighbour(): return lax.ppermute(x, ALL, pairs)  5.94 us
    ppermute x9, waiting for transfers between devices, moved(): return lax.ppermute(x, PLANE, pairs)  5.6 us
    unnamed x4, local copies, waits for them, and re-layouts  2.17 us
    pallas_call x1, Pallas kernels, prepare(): pl.pallas_call(prep_kernel, grid=(1,), in_specs=[pl.BlockSpec(memory_spac...  1.32 us
  transfers between devices with their start and end apart: 10, of which 4 were waited for; matrix products, arithmetic and copies ran while one was open for 0% of the time, Pallas kernels for 12%

profile of v4, /device:TPU:0, one launch (start us, length us, event | category | flops | bytes accessed | tf_op | source)
XLA Modules:
  0.0 60.5 jit_solution(1702447309576052319)
XLA Ops:
  0.0 1.3 %prep.1 = (bf16[256,512]{1,0:T(8,128)(2,1)S(1)}, f32[3,128,128]{2,1,0:T(8,128)S(1)}, bf16[256,256]{1,0:T(8,128)(2,1)S(1)}) custom-call(f32[8,128]{1,0:T(8,128)S(1)} %tick.1.tick_ref, bf16[256,256]{1,0:T(8,128)(2,1)} %source_ref.1, s32[1,128]{1,0:T(1,128)} %bitcast.5, s32[1,128]{1,0:T(1,128)} %bitcast.6, f32[2,128]{1,0:T(2,128)} %quad_ref.1), custom_call_target="tpu_custom_call" | custom-call | tf_op jit(solution)/shard_map/prep/pallas_call | solution.py:98
  1.3 2.2 %copy-done = bf16[1,256,16384]{2,1,0:T(8,128)(2,1)S(1)} copy-done((bf16[1,256,16384]{2,1,0:T(8,128)(2,1)S(1)}, bf16[1,256,16384]{2,1,0:T(8,128)(2,1)}, u32[]{:S(2)}) %copy-start) | copy-done | bytes 8388632
  3.5 3.7 %shard_map.64 = (f32[8,256,256]{2,1,0:T(8,128)S(1)}, bf16[2,2,2,256,1024]{4,3,2,1,0:T(8,128)(2,1)S(1)}) custom-call(bf16[256,512]{1,0:T(8,128)(2,1)S(1)} %get-tuple-element.18.refs_0_, f32[3,128,128]{2,1,0:T(8,128)S(1)} %get-tuple-element.19.refs_1_, bf16[2,256,16384]{2,1,0:T(8,128)(2,1)} %refs_2_.5, bf16[1,256,16384]{2,1,0:T(8,128)(2,1)S(1)} %copy-done), custom_call_target="tpu_custom_call" | custom-call | flops 1610612736 | tf_op jit(solution)/shard_map/pallas_call | solution.py:239
  7.2 0.1 collective-permute-start
  7.3 2.3 %shard_map.65 = (f32[8,256,256]{2,1,0:T(8,128)S(1)}, bf16[2,2,2,256,1024]{4,3,2,1,0:T(8,128)(2,1)S(1)}) custom-call(bf16[256,512]{1,0:T(8,128)(2,1)S(1)} %get-tuple-element.18.refs_0_, f32[3,128,128]{2,1,0:T(8,128)S(1)} %get-tuple-element.19.refs_1_, bf16[2,256,16384]{2,1,0:T(8,128)(2,1)} %refs_2_.5, bf16[1,256,16384]{2,1,0:T(8,128)(2,1)S(1)} %copy-done, ...), custom_call_target="tpu_custom_call" | custom-call | flops 1610612736 | tf_op jit(solution)/shard_map/pallas_call | solution.py:239
  9.6 0.6 collective-permute-start.1
  10.2 0.7 %collective-permute-start.2 = (bf16[256,256]{1,0:T(8,128)(2,1)S(1)}, bf16[256,256]{1,0:T(8,128)(2,1)S(1)}, u32[]{:S(2)}, u32[]{:S(2)}) collective-permute-start(bf16[256,256]{1,0:T(8,128)(2,1)S(1)} %copy-done.1), channel_id=1, source_target_pairs={{32,16},{33,17},{34,18},{35,19},{36,20},{37,21},{38,22},{39,23},{4... | collective-permute-start | bytes 393224 | tf_op jit(solution)/shard_map/ppermute | solution.py:33
  10.8 1.8 %collective-permute-start.3 = (bf16[256,256]{1,0:T(8,128)(2,1)S(1)}, bf16[256,256]{1,0:T(8,128)(2,1)S(1)}, u32[]{:S(2)}, u32[]{:S(2)}) collective-permute-start(bf16[256,256]{1,0:T(8,128)(2,1)S(1)} %copy-done.1), channel_id=1, source_target_pairs={{0,1},{1,2},{2,3},{3,0},{4,5},{5,6},{6,7},{7,4},{8,9},{9,10},{10,1... | collective-permute-start | bytes 393224 | tf_op jit(solution)/shard_map/ppermute | solution.py:33
  12.6 1.5 %collective-permute-start.4 = (bf16[256,256]{1,0:T(8,128)(2,1)S(1)}, bf16[256,256]{1,0:T(8,128)(2,1)S(1)}, u32[]{:S(2)}, u32[]{:S(2)}) collective-permute-start(bf16[256,256]{1,0:T(8,128)(2,1)S(1)} %copy-done.1), channel_id=1, source_target_pairs={{0,3},{1,0},{2,1},{3,2},{4,7},{5,4},{6,5},{7,6},{8,11},{9,8},{10,9... | collective-permute-start | bytes 393224 | tf_op jit(solution)/shard_map/ppermute | solution.py:33
  14.2 2.1 %collective-permute-start.5 = (bf16[256,256]{1,0:T(8,128)(2,1)S(1)}, bf16[256,256]{1,0:T(8,128)(2,1)S(1)}, u32[]{:S(2)}, u32[]{:S(2)}) collective-permute-start(bf16[256,256]{1,0:T(8,128)(2,1)S(1)} %copy-done.1), channel_id=1, source_target_pairs={{0,2},{1,3},{2,0},{3,1},{4,6},{5,7},{6,4},{7,5},{8,10},{9,11},{10,... | collective-permute-start | bytes 393224 | tf_op jit(solution)/shard_map/ppermute | solution.py:33
  16.2 0.8 %collective-permute-done.3.refs_0_ = bf16[256,256]{1,0:T(8,128)(2,1)S(1)} collective-permute-done((bf16[256,256]{1,0:T(8,128)(2,1)S(1)}, bf16[256,256]{1,0:T(8,128)(2,1)S(1)}, u32[]{:S(2)}, u32[]{:S(2)}) %collective-permute-start.3) | collective-permute-done | bytes 131104 | tf_op jit(solution)/shard_map/ppermute | solution.py:33
  17.1 0.5 collective-permute-done.4.refs_1_
  17.6 3.1 %collective-permute-done.5.refs_2_ = bf16[256,256]{1,0:T(8,128)(2,1)S(1)} collective-permute-done((bf16[256,256]{1,0:T(8,128)(2,1)S(1)}, bf16[256,256]{1,0:T(8,128)(2,1)S(1)}, u32[]{:S(2)}, u32[]{:S(2)}) %collective-permute-start.5) | collective-permute-done | bytes 131104 | tf_op jit(solution)/shard_map/ppermute | solution.py:33
  20.7 4.1 %collective-permute-start.8 = (bf16[2,256,256]{2,1,0:T(8,128)(2,1)S(1)}, bf16[2,256,256]{2,1,0:T(8,128)(2,1)S(1)}, u32[]{:S(2)}, u32[]{:S(2)}) collective-permute-start(bf16[2,256,256]{2,1,0:T(8,128)(2,1)S(1)} %get-tuple-element.30), channel_id=1, source_target_pairs={{0,8},{1,9},{2,10},{3,11},{4,12},{5,13},{6,14},{7,15},{8,0},{9,1},... | collective-permute-start | bytes 786440 | tf_op jit(solution)/shard_map/ppermute | solution.py:33
  24.8 1.0 %collective-permute-start.6 = (bf16[4,256,256]{2,1,0:T(8,128)(2,1)S(1)}, bf16[4,256,256]{2,1,0:T(8,128)(2,1)S(1)}, u32[]{:S(2)}, u32[]{:S(2)}) collective-permute-start(bf16[4,256,256]{2,1,0:T(8,128)(2,1)S(1)} %get-tuple-element.26.m_ref), channel_id=1, source_target_pairs={{0,4},{1,5},{2,6},{3,7},{4,8},{5,9},{6,10},{7,11},{8,12},{9,13},{1... | collective-permute-start | bytes 1572872 | tf_op jit(solution)/shard_map/ppermute | solution.py:33
  25.8 2.2 %collective-permute-start.7 = (bf16[4,256,256]{2,1,0:T(8,128)(2,1)S(1)}, bf16[4,256,256]{2,1,0:T(8,128)(2,1)S(1)}, u32[]{:S(2)}, u32[]{:S(2)}) collective-permute-start(bf16[4,256,256]{2,1,0:T(8,128)(2,1)S(1)} %get-tuple-element.26.m_ref), channel_id=1, source_target_pairs={{0,12},{1,13},{2,14},{3,15},{4,0},{5,1},{6,2},{7,3},{8,4},{9,5},{1... | collective-permute-start | bytes 1572872 | tf_op jit(solution)/shard_map/ppermute | solution.py:33
  28.0 1.2 %collective-permute-done.8.here_ref = bf16[2,256,256]{2,1,0:T(8,128)(2,1)S(1)} collective-permute-done((bf16[2,256,256]{2,1,0:T(8,128)(2,1)S(1)}, bf16[2,256,256]{2,1,0:T(8,128)(2,1)S(1)}, u32[]{:S(2)}, u32[]{:S(2)}) %collective-permute-start.8) | collective-permute-done | bytes 262176 | tf_op jit(solution)/shard_map/ppermute | solution.py:33
  29.2 5.9 %collective-permute-start.9 = (bf16[2,256,256]{2,1,0:T(8,128)(2,1)S(1)}, bf16[2,256,256]{2,1,0:T(8,128)(2,1)S(1)}, u32[]{:S(2)}, u32[]{:S(2)}) collective-permute-start(bf16[2,256,256]{2,1,0:T(8,128)(2,1)S(1)} %collective-permute-done.8.here_ref), channel_id=1, source_target_pairs={{0,16},{1,17},{2,18},{3,19},{4,20},{5,21},{6,22},{7,23},{8,24},{9,... | collective-permute-start | bytes 786440 | tf_op jit(solution)/shard_map/ppermute | solution.py:66
  35.1 4.2 %shard_map.66 = (f32[8,256,256]{2,1,0:T(8,128)S(1)}, bf16[2,16,256,256]{3,2,1,0:T(8,128)(2,1)S(1)}) custom-call(bf16[256,512]{1,0:T(8,128)(2,1)S(1)} %get-tuple-element.18.refs_0_, f32[3,128,128]{2,1,0:T(8,128)S(1)} %get-tuple-element.19.refs_1_, bf16[2,256,16384]{2,1,0:T(8,128)(2,1)} %refs_2_.5, bf16[1,256,16384]{2,1,0:T(8,128)(2,1)S(1)} %copy-done, ...), custom_call_target="tpu_custom_call" | custom-call | flops 3221225472 | tf_op jit(solution)/shard_map/pallas_call | solution.py:239
  39.3 1.0 %join.1 = (bf16[2,16,256,256]{3,2,1,0:T(8,128)(2,1)S(1)}, f32[256,256]{1,0:T(8,128)S(1)}) custom-call(f32[8,256,256]{2,1,0:T(8,128)S(1)} %get-tuple-element.23.mine_ref, f32[8,256,256]{2,1,0:T(8,128)S(1)} %collective-permute-done.1.late_ref, bf16[4,256,256]{2,1,0:T(8,128)(2,1)S(1)} %get-tuple-element.26.m_ref, ...), custom_call_target="tpu_custom_call", output_to_operand_aliasing={{0}: (3, {})} | custom-call | flops 2000000000 | tf_op jit(solution)/shard_map/join/pallas_call | solution.py:343
  40.3 1.0 %right.1 = f32[128,256]{1,0:T(8,128)S(1)} custom-call(bf16[2,16,256,256]{3,2,1,0:T(8,128)(2,1)S(1)} %get-tuple-element.28.z_ref, f32[256,256]{1,0:T(8,128)S(1)} %get-tuple-element.29.sum_ref, bf16[4,256,256]{2,1,0:T(8,128)(2,1)S(1)} %collective-permute-done.6.next_ref, bf16[4,256,256]{2,1,0:T(8,128)(2,1)S(1)} %collective-permute-done.7.last_ref, ...), custom_call_target="tpu_custom_call" | custom-call | flops 2000000000 | tf_op jit(solution)/shard_map/right/pallas_call | solution.py:361
  41.3 0.1 copy.8
  41.4 18.3 %all_to_all.5 = f32[128,1,256]{2,1,0:T(1,128)S(1)} all-to-all(f32[128,1,256]{2,1,0:T(1,128)S(1)} %copy.8), channel_id=1, replica_groups=mesh['xh'=2,'c'=2,'xl'=2,'z'=4,'y'=4] {'xh','c','xl','z','y'}, dimensions={0} | all-to-all | bytes 262144 | tf_op jit(solution)/shard_map/all_to_all | solution.py:407
  59.8 0.7 %reduce_sum.11 = f32[256]{0:T(256)} reduce(f32[128,1,256]{2,1,0:T(1,128)S(1)} %all_to_all.5, f32[]{:T(128)} %constant.0.clone.1), dimensions={0,1}, to_apply=%region_0.0 | reduce | flops 32512 | bytes 132100 | tf_op jit(solution)/shard_map/reduce_sum | solution.py:408
  (11 shorter events, 0.1 us)
Async XLA Ops:
  0.0 3.5 %copy-start = (bf16[1,256,16384]{2,1,0:T(8,128)(2,1)S(1)}, bf16[1,256,16384]{2,1,0:T(8,128)(2,1)}, u32[]{:S(2)}) copy-start(bf16[1,256,16384]{2,1,0:T(8,128)(2,1)} %refs_3_.5) | copy-start | bytes 25165828
  7.2 27.9 %collective-permute-start = (f32[8,256,256]{2,1,0:T(8,128)S(1)}, f32[8,256,256]{2,1,0:T(8,128)S(1)}, u32[]{:S(2)}, u32[]{:S(2)}) collective-permute-start(f32[8,256,256]{2,1,0:T(8,128)S(1)} %get-tuple-element.22), channel_id=1, source_target_pairs={{0,32},{1,33},{2,34},{3,35},{4,36},{5,37},{6,38},{7,39},{8,40},{9,... | collective-permute-start | bytes 6291464 | tf_op jit(solution)/shard_map/ppermute | solution.py:33
  7.3 2.8 %copy-start.1 = (bf16[256,256]{1,0:T(8,128)(2,1)S(1)}, bf16[256,256]{1,0:T(8,128)(2,1)}, u32[]{:S(2)}) copy-start(bf16[256,256]{1,0:T(8,128)(2,1)} %source_ref.1) | copy-start | bytes 393220
  9.6 29.7 %collective-permute-start.1 = (f32[8,256,256]{2,1,0:T(8,128)S(1)}, f32[8,256,256]{2,1,0:T(8,128)S(1)}, u32[]{:S(2)}, u32[]{:S(2)}) collective-permute-start(f32[8,256,256]{2,1,0:T(8,128)S(1)} %get-tuple-element.24), channel_id=1, source_target_pairs={{0,32},{1,33},{2,34},{3,35},{4,36},{5,37},{6,38},{7,39},{8,40},{9,... | collective-permute-start | bytes 6291464 | tf_op jit(solution)/shard_map/ppermute | solution.py:33
  10.2 4.0 %collective-permute-start.2 = (bf16[256,256]{1,0:T(8,128)(2,1)S(1)}, bf16[256,256]{1,0:T(8,128)(2,1)S(1)}, u32[]{:S(2)}, u32[]{:S(2)}) collective-permute-start(bf16[256,256]{1,0:T(8,128)(2,1)S(1)} %copy-done.1), channel_id=1, source_target_pairs={{32,16},{33,17},{34,18},{35,19},{36,20},{37,21},{38,22},{39,23},{4... | collective-permute-start | bytes 393224 | tf_op jit(solution)/shard_map/ppermute | solution.py:33
  10.8 6.2 %collective-permute-start.3 = (bf16[256,256]{1,0:T(8,128)(2,1)S(1)}, bf16[256,256]{1,0:T(8,128)(2,1)S(1)}, u32[]{:S(2)}, u32[]{:S(2)}) collective-permute-start(bf16[256,256]{1,0:T(8,128)(2,1)S(1)} %copy-done.1), channel_id=1, source_target_pairs={{0,1},{1,2},{2,3},{3,0},{4,5},{5,6},{6,7},{7,4},{8,9},{9,10},{10,1... | collective-permute-start | bytes 393224 | tf_op jit(solution)/shard_map/ppermute | solution.py:33
  12.6 5.0 %collective-permute-start.4 = (bf16[256,256]{1,0:T(8,128)(2,1)S(1)}, bf16[256,256]{1,0:T(8,128)(2,1)S(1)}, u32[]{:S(2)}, u32[]{:S(2)}) collective-permute-start(bf16[256,256]{1,0:T(8,128)(2,1)S(1)} %copy-done.1), channel_id=1, source_target_pairs={{0,3},{1,0},{2,1},{3,2},{4,7},{5,4},{6,5},{7,6},{8,11},{9,8},{10,9... | collective-permute-start | bytes 393224 | tf_op jit(solution)/shard_map/ppermute | solution.py:33
  14.2 6.5 %collective-permute-start.5 = (bf16[256,256]{1,0:T(8,128)(2,1)S(1)}, bf16[256,256]{1,0:T(8,128)(2,1)S(1)}, u32[]{:S(2)}, u32[]{:S(2)}) collective-permute-start(bf16[256,256]{1,0:T(8,128)(2,1)S(1)} %copy-done.1), channel_id=1, source_target_pairs={{0,2},{1,3},{2,0},{3,1},{4,6},{5,7},{6,4},{7,5},{8,10},{9,11},{10,... | collective-permute-start | bytes 393224 | tf_op jit(solution)/shard_map/ppermute | solution.py:33
  20.7 8.5 %collective-permute-start.8 = (bf16[2,256,256]{2,1,0:T(8,128)(2,1)S(1)}, bf16[2,256,256]{2,1,0:T(8,128)(2,1)S(1)}, u32[]{:S(2)}, u32[]{:S(2)}) collective-permute-start(bf16[2,256,256]{2,1,0:T(8,128)(2,1)S(1)} %get-tuple-element.30), channel_id=1, source_target_pairs={{0,8},{1,9},{2,10},{3,11},{4,12},{5,13},{6,14},{7,15},{8,0},{9,1},... | collective-permute-start | bytes 786440 | tf_op jit(solution)/shard_map/ppermute | solution.py:33
  24.8 15.5 %collective-permute-start.6 = (bf16[4,256,256]{2,1,0:T(8,128)(2,1)S(1)}, bf16[4,256,256]{2,1,0:T(8,128)(2,1)S(1)}, u32[]{:S(2)}, u32[]{:S(2)}) collective-permute-start(bf16[4,256,256]{2,1,0:T(8,128)(2,1)S(1)} %get-tuple-element.26.m_ref), channel_id=1, source_target_pairs={{0,4},{1,5},{2,6},{3,7},{4,8},{5,9},{6,10},{7,11},{8,12},{9,13},{1... | collective-permute-start | bytes 1572872 | tf_op jit(solution)/shard_map/ppermute | solution.py:33
  25.8 14.5 %collective-permute-start.7 = (bf16[4,256,256]{2,1,0:T(8,128)(2,1)S(1)}, bf16[4,256,256]{2,1,0:T(8,128)(2,1)S(1)}, u32[]{:S(2)}, u32[]{:S(2)}) collective-permute-start(bf16[4,256,256]{2,1,0:T(8,128)(2,1)S(1)} %get-tuple-element.26.m_ref), channel_id=1, source_target_pairs={{0,12},{1,13},{2,14},{3,15},{4,0},{5,1},{6,2},{7,3},{8,4},{9,5},{1... | collective-permute-start | bytes 1572872 | tf_op jit(solution)/shard_map/ppermute | solution.py:33
  29.2 11.1 %collective-permute-start.9 = (bf16[2,256,256]{2,1,0:T(8,128)(2,1)S(1)}, bf16[2,256,256]{2,1,0:T(8,128)(2,1)S(1)}, u32[]{:S(2)}, u32[]{:S(2)}) collective-permute-start(bf16[2,256,256]{2,1,0:T(8,128)(2,1)S(1)} %collective-permute-done.8.here_ref), channel_id=1, source_target_pairs={{0,16},{1,17},{2,18},{3,19},{4,20},{5,21},{6,22},{7,23},{8,24},{9,... | collective-permute-start | bytes 786440 | tf_op jit(solution)/shard_map/ppermute | solution.py:66

commit v5 on v4

--- a/solution.py
+++ b/solution.py
@@ -367,6 +367,21 @@
         compiler_params=pltpu.CompilerParams(vmem_limit_bytes=4 * 2**20),
         name="right",
     )(*args)
+
+
+def add_up_kernel(parts_ref, out_ref):
+    out_ref[...] = jnp.sum(parts_ref[...], axis=0)
+
+
+def add_up(parts):
+    return pl.pallas_call(
+        add_up_kernel,
+        in_specs=[pl.BlockSpec(memory_space=pltpu.VMEM)],
+        out_specs=pl.BlockSpec(memory_space=pltpu.VMEM),
+        out_shape=jax.ShapeDtypeStruct(parts.shape[1:], parts.dtype),
+        compiler_params=pltpu.CompilerParams(vmem_limit_bytes=4 * 2**20),
+        name="add_up",
+    )(parts)
 
 
 def on_device(w_imag, w_real, pair_elements, quad_weight, residue_freq, owner_bands):
@@ -405,7 +420,7 @@
     n_dev = 128
     parts = total.reshape(n_dev, 1, 2 * bands)
     arrived = lax.all_to_all(parts, ALL, split_axis=0, concat_axis=0, tiled=True)
-    return arrived.sum(axis=0)
+    return add_up(arrived)
 
 
 def solution(mesh):

time: 61.3 us -> 61.2 us (level)
  other arithmetic: 0.71 us -> 0 us
  Pallas kernels: 13.5 us -> 14.2 us
    reduce_sum x1 -> x0, other arithmetic: 0.71 us -> none  [on_device(): return arrived.sum(axis=0)]
    pallas_call x0 -> x1, Pallas kernels: none -> 0.71 us  [add_up(): pl.pallas_call(add_up_kernel, in_specs=[pl.BlockSpec(memory_space=pltpu.V...]
where the time goes in v5:
time: 61.2 us; the launch traced here: 60.4 us
  starting transfers between devices  19.9 us (33%)
  blocking collectives  18.3 us (30%)
  Pallas kernels  14.2 us (23%)
  waiting for transfers between devices  5.61 us (9%)
  local copies, waits for them, and re-layouts  2.26 us (4%)
    all_to_all x1, blocking collectives, on_device(): lax.all_to_all(parts, ALL, split_axis=0, concat_axis=0, tiled=True)  18.3 us
    ppermute x9, starting transfers between devices, moved(): return lax.ppermute(x, PLANE, pairs)  14 us
    pallas_call x3, Pallas kernels, left(): pl.pallas_call(functools.partial(left_kernel, job=job), in_specs=in_specs...  10.2 us
    ppermute x1, starting transfers between devices, x_neighbour(): return lax.ppermute(x, ALL, pairs)  5.94 us
    ppermute x9, waiting for transfers between devices, moved(): return lax.ppermute(x, PLANE, pairs)  5.6 us
    unnamed x4, local copies, waits for them, and re-layouts  2.17 us
    pallas_call x1, Pallas kernels, prepare(): pl.pallas_call(prep_kernel, grid=(1,), in_specs=[pl.BlockSpec(memory_spac...  1.32 us
  transfers between devices with their start and end apart: 10, of which 4 were waited for; matrix products, arithmetic and copies ran while one was open for 0% of the time, Pallas kernels for 12%

profile of v5, /device:TPU:0, one launch (start us, length us, event | category | flops | bytes accessed | tf_op | source)
XLA Modules:
  0.0 60.4 jit_solution(11200129607034850701)
XLA Ops:
  0.0 1.3 %prep.1 = (bf16[256,512]{1,0:T(8,128)(2,1)S(1)}, f32[3,128,128]{2,1,0:T(8,128)S(1)}, bf16[256,256]{1,0:T(8,128)(2,1)S(1)}) custom-call(f32[8,128]{1,0:T(8,128)S(1)} %tick.1.tick_ref, bf16[256,256]{1,0:T(8,128)(2,1)} %source_ref.1, s32[1,128]{1,0:T(1,128)} %bitcast.2, s32[1,128]{1,0:T(1,128)} %bitcast.3, f32[2,128]{1,0:T(2,128)} %quad_ref.1), custom_call_target="tpu_custom_call" | custom-call | tf_op jit(solution)/shard_map/prep/pallas_call | solution.py:98
  1.3 2.2 %copy-done = bf16[1,256,16384]{2,1,0:T(8,128)(2,1)S(1)} copy-done((bf16[1,256,16384]{2,1,0:T(8,128)(2,1)S(1)}, bf16[1,256,16384]{2,1,0:T(8,128)(2,1)}, u32[]{:S(2)}) %copy-start) | copy-done | bytes 8388632
  3.5 3.7 %shard_map.64 = (f32[8,256,256]{2,1,0:T(8,128)S(1)}, bf16[2,2,2,256,1024]{4,3,2,1,0:T(8,128)(2,1)S(1)}) custom-call(bf16[256,512]{1,0:T(8,128)(2,1)S(1)} %get-tuple-element.18.refs_0_, f32[3,128,128]{2,1,0:T(8,128)S(1)} %get-tuple-element.19.refs_1_, bf16[2,256,16384]{2,1,0:T(8,128)(2,1)} %refs_2_.5, bf16[1,256,16384]{2,1,0:T(8,128)(2,1)S(1)} %copy-done), custom_call_target="tpu_custom_call" | custom-call | flops 1610612736 | tf_op jit(solution)/shard_map/pallas_call | solution.py:239
  7.2 0.1 collective-permute-start
  7.3 2.3 %shard_map.65 = (f32[8,256,256]{2,1,0:T(8,128)S(1)}, bf16[2,2,2,256,1024]{4,3,2,1,0:T(8,128)(2,1)S(1)}) custom-call(bf16[256,512]{1,0:T(8,128)(2,1)S(1)} %get-tuple-element.18.refs_0_, f32[3,128,128]{2,1,0:T(8,128)S(1)} %get-tuple-element.19.refs_1_, bf16[2,256,16384]{2,1,0:T(8,128)(2,1)} %refs_2_.5, bf16[1,256,16384]{2,1,0:T(8,128)(2,1)S(1)} %copy-done, ...), custom_call_target="tpu_custom_call" | custom-call | flops 1610612736 | tf_op jit(solution)/shard_map/pallas_call | solution.py:239
  9.6 0.6 collective-permute-start.1
  10.2 0.7 %collective-permute-start.2 = (bf16[256,256]{1,0:T(8,128)(2,1)S(1)}, bf16[256,256]{1,0:T(8,128)(2,1)S(1)}, u32[]{:S(2)}, u32[]{:S(2)}) collective-permute-start(bf16[256,256]{1,0:T(8,128)(2,1)S(1)} %copy-done.1), channel_id=1, source_target_pairs={{32,16},{33,17},{34,18},{35,19},{36,20},{37,21},{38,22},{39,23},{4... | collective-permute-start | bytes 393224 | tf_op jit(solution)/shard_map/ppermute | solution.py:33
  10.8 1.8 %collective-permute-start.3 = (bf16[256,256]{1,0:T(8,128)(2,1)S(1)}, bf16[256,256]{1,0:T(8,128)(2,1)S(1)}, u32[]{:S(2)}, u32[]{:S(2)}) collective-permute-start(bf16[256,256]{1,0:T(8,128)(2,1)S(1)} %copy-done.1), channel_id=1, source_target_pairs={{0,1},{1,2},{2,3},{3,0},{4,5},{5,6},{6,7},{7,4},{8,9},{9,10},{10,1... | collective-permute-start | bytes 393224 | tf_op jit(solution)/shard_map/ppermute | solution.py:33
  12.6 1.5 %collective-permute-start.4 = (bf16[256,256]{1,0:T(8,128)(2,1)S(1)}, bf16[256,256]{1,0:T(8,128)(2,1)S(1)}, u32[]{:S(2)}, u32[]{:S(2)}) collective-permute-start(bf16[256,256]{1,0:T(8,128)(2,1)S(1)} %copy-done.1), channel_id=1, source_target_pairs={{0,3},{1,0},{2,1},{3,2},{4,7},{5,4},{6,5},{7,6},{8,11},{9,8},{10,9... | collective-permute-start | bytes 393224 | tf_op jit(solution)/shard_map/ppermute | solution.py:33
  14.2 2.1 %collective-permute-start.5 = (bf16[256,256]{1,0:T(8,128)(2,1)S(1)}, bf16[256,256]{1,0:T(8,128)(2,1)S(1)}, u32[]{:S(2)}, u32[]{:S(2)}) collective-permute-start(bf16[256,256]{1,0:T(8,128)(2,1)S(1)} %copy-done.1), channel_id=1, source_target_pairs={{0,2},{1,3},{2,0},{3,1},{4,6},{5,7},{6,4},{7,5},{8,10},{9,11},{10,... | collective-permute-start | bytes 393224 | tf_op jit(solution)/shard_map/ppermute | solution.py:33
  16.2 0.8 %collective-permute-done.3.refs_0_ = bf16[256,256]{1,0:T(8,128)(2,1)S(1)} collective-permute-done((bf16[256,256]{1,0:T(8,128)(2,1)S(1)}, bf16[256,256]{1,0:T(8,128)(2,1)S(1)}, u32[]{:S(2)}, u32[]{:S(2)}) %collective-permute-start.3) | collective-permute-done | bytes 131104 | tf_op jit(solution)/shard_map/ppermute | solution.py:33
  17.1 0.5 collective-permute-done.4.refs_1_
  17.6 3.1 %collective-permute-done.5.refs_2_ = bf16[256,256]{1,0:T(8,128)(2,1)S(1)} collective-permute-done((bf16[256,256]{1,0:T(8,128)(2,1)S(1)}, bf16[256,256]{1,0:T(8,128)(2,1)S(1)}, u32[]{:S(2)}, u32[]{:S(2)}) %collective-permute-start.5) | collective-permute-done | bytes 131104 | tf_op jit(solution)/shard_map/ppermute | solution.py:33
  20.7 4.1 %collective-permute-start.8 = (bf16[2,256,256]{2,1,0:T(8,128)(2,1)S(1)}, bf16[2,256,256]{2,1,0:T(8,128)(2,1)S(1)}, u32[]{:S(2)}, u32[]{:S(2)}) collective-permute-start(bf16[2,256,256]{2,1,0:T(8,128)(2,1)S(1)} %get-tuple-element.30), channel_id=1, source_target_pairs={{0,8},{1,9},{2,10},{3,11},{4,12},{5,13},{6,14},{7,15},{8,0},{9,1},... | collective-permute-start | bytes 786440 | tf_op jit(solution)/shard_map/ppermute | solution.py:33
  24.8 1.0 %collective-permute-start.6 = (bf16[4,256,256]{2,1,0:T(8,128)(2,1)S(1)}, bf16[4,256,256]{2,1,0:T(8,128)(2,1)S(1)}, u32[]{:S(2)}, u32[]{:S(2)}) collective-permute-start(bf16[4,256,256]{2,1,0:T(8,128)(2,1)S(1)} %get-tuple-element.26.m_ref), channel_id=1, source_target_pairs={{0,4},{1,5},{2,6},{3,7},{4,8},{5,9},{6,10},{7,11},{8,12},{9,13},{1... | collective-permute-start | bytes 1572872 | tf_op jit(solution)/shard_map/ppermute | solution.py:33
  25.8 2.2 %collective-permute-start.7 = (bf16[4,256,256]{2,1,0:T(8,128)(2,1)S(1)}, bf16[4,256,256]{2,1,0:T(8,128)(2,1)S(1)}, u32[]{:S(2)}, u32[]{:S(2)}) collective-permute-start(bf16[4,256,256]{2,1,0:T(8,128)(2,1)S(1)} %get-tuple-element.26.m_ref), channel_id=1, source_target_pairs={{0,12},{1,13},{2,14},{3,15},{4,0},{5,1},{6,2},{7,3},{8,4},{9,5},{1... | collective-permute-start | bytes 1572872 | tf_op jit(solution)/shard_map/ppermute | solution.py:33
  28.0 1.2 %collective-permute-done.8.here_ref = bf16[2,256,256]{2,1,0:T(8,128)(2,1)S(1)} collective-permute-done((bf16[2,256,256]{2,1,0:T(8,128)(2,1)S(1)}, bf16[2,256,256]{2,1,0:T(8,128)(2,1)S(1)}, u32[]{:S(2)}, u32[]{:S(2)}) %collective-permute-start.8) | collective-permute-done | bytes 262176 | tf_op jit(solution)/shard_map/ppermute | solution.py:33
  29.2 5.9 %collective-permute-start.9 = (bf16[2,256,256]{2,1,0:T(8,128)(2,1)S(1)}, bf16[2,256,256]{2,1,0:T(8,128)(2,1)S(1)}, u32[]{:S(2)}, u32[]{:S(2)}) collective-permute-start(bf16[2,256,256]{2,1,0:T(8,128)(2,1)S(1)} %collective-permute-done.8.here_ref), channel_id=1, source_target_pairs={{0,16},{1,17},{2,18},{3,19},{4,20},{5,21},{6,22},{7,23},{8,24},{9,... | collective-permute-start | bytes 786440 | tf_op jit(solution)/shard_map/ppermute | solution.py:66
  35.1 4.2 %shard_map.66 = (f32[8,256,256]{2,1,0:T(8,128)S(1)}, bf16[2,16,256,256]{3,2,1,0:T(8,128)(2,1)S(1)}) custom-call(bf16[256,512]{1,0:T(8,128)(2,1)S(1)} %get-tuple-element.18.refs_0_, f32[3,128,128]{2,1,0:T(8,128)S(1)} %get-tuple-element.19.refs_1_, bf16[2,256,16384]{2,1,0:T(8,128)(2,1)} %refs_2_.5, bf16[1,256,16384]{2,1,0:T(8,128)(2,1)S(1)} %copy-done, ...), custom_call_target="tpu_custom_call" | custom-call | flops 3221225472 | tf_op jit(solution)/shard_map/pallas_call | solution.py:239
  39.3 1.0 %join.1 = (bf16[2,16,256,256]{3,2,1,0:T(8,128)(2,1)S(1)}, f32[256,256]{1,0:T(8,128)S(1)}) custom-call(f32[8,256,256]{2,1,0:T(8,128)S(1)} %get-tuple-element.23.mine_ref, f32[8,256,256]{2,1,0:T(8,128)S(1)} %collective-permute-done.1.late_ref, bf16[4,256,256]{2,1,0:T(8,128)(2,1)S(1)} %get-tuple-element.26.m_ref, ...), custom_call_target="tpu_custom_call", output_to_operand_aliasing={{0}: (3, {})} | custom-call | flops 2000000000 | tf_op jit(solution)/shard_map/join/pallas_call | solution.py:343
  40.3 1.0 %right.1 = f32[128,256]{1,0:T(8,128)S(1)} custom-call(bf16[2,16,256,256]{3,2,1,0:T(8,128)(2,1)S(1)} %get-tuple-element.28.z_ref, f32[256,256]{1,0:T(8,128)S(1)} %get-tuple-element.29.sum_ref, bf16[4,256,256]{2,1,0:T(8,128)(2,1)S(1)} %collective-permute-done.6.next_ref, bf16[4,256,256]{2,1,0:T(8,128)(2,1)S(1)} %collective-permute-done.7.last_ref, ...), custom_call_target="tpu_custom_call" | custom-call | flops 2000000000 | tf_op jit(solution)/shard_map/right/pallas_call | solution.py:361
  41.3 0.1 reshape.11
  41.4 18.3 %all_to_all.5.parts_ref = f32[128,1,256]{2,1,0:T(1,128)S(1)} all-to-all(f32[128,1,256]{2,1,0:T(1,128)S(1)} %reshape.11), channel_id=1, replica_groups=mesh['xh'=2,'c'=2,'xl'=2,'z'=4,'y'=4] {'xh','c','xl','z','y'}, dimensions={0} | all-to-all | bytes 262144 | tf_op jit(solution)/shard_map/all_to_all | solution.py:422
  59.7 0.7 %add_up.1 = f32[1,256]{1,0:T(1,128)} custom-call(f32[128,1,256]{2,1,0:T(1,128)S(1)} %all_to_all.5.parts_ref), custom_call_target="tpu_custom_call" | custom-call | tf_op jit(solution)/shard_map/add_up/pallas_call | solution.py:377
  (11 shorter events, 0.1 us)
Async XLA Ops:
  0.0 3.5 %copy-start = (bf16[1,256,16384]{2,1,0:T(8,128)(2,1)S(1)}, bf16[1,256,16384]{2,1,0:T(8,128)(2,1)}, u32[]{:S(2)}) copy-start(bf16[1,256,16384]{2,1,0:T(8,128)(2,1)} %refs_3_.5) | copy-start | bytes 25165828
  7.2 27.9 %collective-permute-start = (f32[8,256,256]{2,1,0:T(8,128)S(1)}, f32[8,256,256]{2,1,0:T(8,128)S(1)}, u32[]{:S(2)}, u32[]{:S(2)}) collective-permute-start(f32[8,256,256]{2,1,0:T(8,128)S(1)} %get-tuple-element.22), channel_id=1, source_target_pairs={{0,32},{1,33},{2,34},{3,35},{4,36},{5,37},{6,38},{7,39},{8,40},{9,... | collective-permute-start | bytes 6291464 | tf_op jit(solution)/shard_map/ppermute | solution.py:33
  7.3 2.8 %copy-start.1 = (bf16[256,256]{1,0:T(8,128)(2,1)S(1)}, bf16[256,256]{1,0:T(8,128)(2,1)}, u32[]{:S(2)}) copy-start(bf16[256,256]{1,0:T(8,128)(2,1)} %source_ref.1) | copy-start | bytes 393220
  9.6 29.7 %collective-permute-start.1 = (f32[8,256,256]{2,1,0:T(8,128)S(1)}, f32[8,256,256]{2,1,0:T(8,128)S(1)}, u32[]{:S(2)}, u32[]{:S(2)}) collective-permute-start(f32[8,256,256]{2,1,0:T(8,128)S(1)} %get-tuple-element.24), channel_id=1, source_target_pairs={{0,32},{1,33},{2,34},{3,35},{4,36},{5,37},{6,38},{7,39},{8,40},{9,... | collective-permute-start | bytes 6291464 | tf_op jit(solution)/shard_map/ppermute | solution.py:33
  10.2 4.0 %collective-permute-start.2 = (bf16[256,256]{1,0:T(8,128)(2,1)S(1)}, bf16[256,256]{1,0:T(8,128)(2,1)S(1)}, u32[]{:S(2)}, u32[]{:S(2)}) collective-permute-start(bf16[256,256]{1,0:T(8,128)(2,1)S(1)} %copy-done.1), channel_id=1, source_target_pairs={{32,16},{33,17},{34,18},{35,19},{36,20},{37,21},{38,22},{39,23},{4... | collective-permute-start | bytes 393224 | tf_op jit(solution)/shard_map/ppermute | solution.py:33
  10.8 6.2 %collective-permute-start.3 = (bf16[256,256]{1,0:T(8,128)(2,1)S(1)}, bf16[256,256]{1,0:T(8,128)(2,1)S(1)}, u32[]{:S(2)}, u32[]{:S(2)}) collective-permute-start(bf16[256,256]{1,0:T(8,128)(2,1)S(1)} %copy-done.1), channel_id=1, source_target_pairs={{0,1},{1,2},{2,3},{3,0},{4,5},{5,6},{6,7},{7,4},{8,9},{9,10},{10,1... | collective-permute-start | bytes 393224 | tf_op jit(solution)/shard_map/ppermute | solution.py:33
  12.6 5.0 %collective-permute-start.4 = (bf16[256,256]{1,0:T(8,128)(2,1)S(1)}, bf16[256,256]{1,0:T(8,128)(2,1)S(1)}, u32[]{:S(2)}, u32[]{:S(2)}) collective-permute-start(bf16[256,256]{1,0:T(8,128)(2,1)S(1)} %copy-done.1), channel_id=1, source_target_pairs={{0,3},{1,0},{2,1},{3,2},{4,7},{5,4},{6,5},{7,6},{8,11},{9,8},{10,9... | collective-permute-start | bytes 393224 | tf_op jit(solution)/shard_map/ppermute | solution.py:33
  14.2 6.5 %collective-permute-start.5 = (bf16[256,256]{1,0:T(8,128)(2,1)S(1)}, bf16[256,256]{1,0:T(8,128)(2,1)S(1)}, u32[]{:S(2)}, u32[]{:S(2)}) collective-permute-start(bf16[256,256]{1,0:T(8,128)(2,1)S(1)} %copy-done.1), channel_id=1, source_target_pairs={{0,2},{1,3},{2,0},{3,1},{4,6},{5,7},{6,4},{7,5},{8,10},{9,11},{10,... | collective-permute-start | bytes 393224 | tf_op jit(solution)/shard_map/ppermute | solution.py:33
  20.7 8.5 %collective-permute-start.8 = (bf16[2,256,256]{2,1,0:T(8,128)(2,1)S(1)}, bf16[2,256,256]{2,1,0:T(8,128)(2,1)S(1)}, u32[]{:S(2)}, u32[]{:S(2)}) collective-permute-start(bf16[2,256,256]{2,1,0:T(8,128)(2,1)S(1)} %get-tuple-element.30), channel_id=1, source_target_pairs={{0,8},{1,9},{2,10},{3,11},{4,12},{5,13},{6,14},{7,15},{8,0},{9,1},... | collective-permute-start | bytes 786440 | tf_op jit(solution)/shard_map/ppermute | solution.py:33
  24.8 15.5 %collective-permute-start.6 = (bf16[4,256,256]{2,1,0:T(8,128)(2,1)S(1)}, bf16[4,256,256]{2,1,0:T(8,128)(2,1)S(1)}, u32[]{:S(2)}, u32[]{:S(2)}) collective-permute-start(bf16[4,256,256]{2,1,0:T(8,128)(2,1)S(1)} %get-tuple-element.26.m_ref), channel_id=1, source_target_pairs={{0,4},{1,5},{2,6},{3,7},{4,8},{5,9},{6,10},{7,11},{8,12},{9,13},{1... | collective-permute-start | bytes 1572872 | tf_op jit(solution)/shard_map/ppermute | solution.py:33
  25.8 14.5 %collective-permute-start.7 = (bf16[4,256,256]{2,1,0:T(8,128)(2,1)S(1)}, bf16[4,256,256]{2,1,0:T(8,128)(2,1)S(1)}, u32[]{:S(2)}, u32[]{:S(2)}) collective-permute-start(bf16[4,256,256]{2,1,0:T(8,128)(2,1)S(1)} %get-tuple-element.26.m_ref), channel_id=1, source_target_pairs={{0,12},{1,13},{2,14},{3,15},{4,0},{5,1},{6,2},{7,3},{8,4},{9,5},{1... | collective-permute-start | bytes 1572872 | tf_op jit(solution)/shard_map/ppermute | solution.py:33
  29.2 11.1 %collective-permute-start.9 = (bf16[2,256,256]{2,1,0:T(8,128)(2,1)S(1)}, bf16[2,256,256]{2,1,0:T(8,128)(2,1)S(1)}, u32[]{:S(2)}, u32[]{:S(2)}) collective-permute-start(bf16[2,256,256]{2,1,0:T(8,128)(2,1)S(1)} %collective-permute-done.8.here_ref), channel_id=1, source_target_pairs={{0,16},{1,17},{2,18},{3,19},{4,20},{5,21},{6,22},{7,23},{8,24},{9,... | collective-permute-start | bytes 786440 | tf_op jit(solution)/shard_map/ppermute | solution.py:66
